TPU v7x, 32 devices: a whole 2x2x4 slice. The times are simulated.
32 devices in a mesh: gx: 4 (over z), gy: 4 (over x, core), gz: 2 (over y).
Axes of the slice: x: 2, y: 2, z: 4, core: 2. Of those that a mesh axis runs over, the one named last changes fastest.
Arguments:
- x_a: bfloat16 [32, 8, 64, 256], P(None, 'gx', 'gy', 'gz'), may hold values from -12 to 12
- x_b: bfloat16 [32, 8, 64, 256], P(None, 'gx', 'gy', 'gz'), may hold values from -12 to 12
- w_first: bfloat16 [3, 3, 3, 32, 32], replicated, may hold values from -0.21875 to 0.21875
- w_second: bfloat16 [3, 3, 3, 32, 32], replicated, may hold values from -0.21875 to 0.21875
- gain_first: float32 [32], replicated, may hold values from 0.1 to 1.9
- bias_first: float32 [32], replicated, may hold values from -2 to 2
- gain_second: float32 [32], replicated, may hold values from 0.1 to 1.9
- bias_second: float32 [32], replicated, may hold values from -2 to 2
- grad_out: bfloat16 [32, 8, 64, 256], P(None, 'gx', 'gy', 'gz'), may hold values from -6 to 6
Outputs:
- y_a: bfloat16 [32, 8, 64, 256], P(None, 'gx', 'gy', 'gz')
- dx_b: bfloat16 [32, 8, 64, 256], P(None, 'gx', 'gy', 'gz')
- grad_w_first: float32 [3, 3, 3, 32, 32], replicated
- grad_w_second: float32 [3, 3, 3, 32, 32], replicated
- grad_norm: float32 [4, 32], replicated
All inputs are finite; a program needn't handle non-finite values.
Results may differ from a plain program's by a relative error of at most 0.0063.
Values may be sent and summed in bfloat16 or wider, within the bound.
A program may use at most 128 MiB of HBM per device.

v0:
```python
import functools
import math

import jax
import jax.numpy as jnp
from jax import lax
from jax.experimental import pallas as pl
from jax.experimental.pallas import tpu as pltpu
from jax.sharding import PartitionSpec as P

EPSILON = 1e-05
AXES = ("gx", "gy", "gz")
MESH = pl.DeviceIdType.MESH


def slope_of(z):
    s = jax.nn.sigmoid(z)
    return s * (1.0 + z * (1.0 - s))


def kernel(
    sizes, voxels,
    xa, xb, go, w1, w2, w1t, w2t, g1, b1, g2, b2,
    ya, dxb, gw1, gw2, gnorm,
    pads, edge_out, edge_in, edge_x, bases, shift_a, shift_xb, shift_hb, shift_d,
    c1a, c1b, c2a, c2b, d2, d1, stat, wbuf, wacc,
    halo_send, halo_recv, sum_send, sum_recv, w_send, w_recv,
):
    nx, ny, chan, nz = xa.shape
    half = ny // 2
    wide = ny + 2
    me = [lax.axis_index(a) for a in AXES]
    factor = 1.0 / math.sqrt(voxels)
    lane = lax.broadcasted_iota(jnp.int32, (chan, nz), 1)
    zero = jnp.zeros((chan, nz), jnp.float32)

    counts = (sizes[0], sizes[1] * sizes[2])
    rank = (me[0], me[1] * sizes[2] + me[2])

    def peers(k):
        n = counts[k]
        return [(lax.rem(rank[k] + d, n), lax.rem(rank[k] + n - d, n)) for d in range(1, n)]

    def where(k, at):
        if k == 0:
            return {AXES[0]: at}
        return {AXES[1]: at // sizes[2], AXES[2]: at % sizes[2]}

    barrier = pltpu.get_barrier_semaphore()
    count = 0
    for k in range(2):
        for to, _ in peers(k):
            pl.semaphore_signal(barrier, inc=1, device_id=where(k, to), device_id_type=MESH)
            count += 1
    pl.semaphore_wait(barrier, count)

    def halo_refs(v, k):
        p = pads.at[v]
        if k == 0:
            rows = pl.ds(1, ny)
            return (p.at[nx, rows], p.at[0, rows]), (p.at[1, rows], p.at[nx + 1, rows])
        if k == 1:
            rows = pl.ds(1, nx)
            return (p.at[rows, ny], p.at[rows, 0]), (p.at[rows, 1], p.at[rows, ny + 1])
        if k == 3 or k == 4:
            y = 0 if k == 3 else ny + 1
            return (p.at[nx, y], p.at[0, y]), (p.at[1, y], p.at[nx + 1, y])
        if k == 5:
            return (edge_in.at[v], edge_x.at[v, 0]), (edge_in.at[v], edge_x.at[v, 1])
        return (edge_out.at[v, 0], edge_in.at[v, 0]), (edge_out.at[v, 1], edge_in.at[v, 1])

    def halo_copy(v, k, side):
        src, dst = halo_refs(v, k)[side]
        return pltpu.make_async_remote_copy(
            src_ref=src, dst_ref=dst, send_sem=halo_send.at[v, k, side],
            recv_sem=halo_recv.at[v, k, side], device_id={AXES[along[k]]: me[along[k]] + 1 - 2 * side},
            device_id_type=MESH)

    along = (0, 1, 2, 0, 0, 0)

    def halo_start(v, k):
        here, n = me[along[k]], sizes[along[k]]
        (_, up_dst), (_, down_dst) = halo_refs(v, k)

        @pl.when(here < n - 1)
        def _():
            halo_copy(v, k, 0).start()

        @pl.when(here > 0)
        def _():
            halo_copy(v, k, 1).start()

        @pl.when(here == 0)
        def _():
            up_dst[...] = jnp.zeros(up_dst.shape, up_dst.dtype)

        @pl.when(here == n - 1)
        def _():
            down_dst[...] = jnp.zeros(down_dst.shape, down_dst.dtype)

    def halo_wait(v, k):
        here, n = me[along[k]], sizes[along[k]]

        @pl.when(here < n - 1)
        def _():
            halo_copy(v, k, 0).wait_send()
            halo_copy(v, k, 1).wait_recv()

        @pl.when(here > 0)
        def _():
            halo_copy(v, k, 1).wait_send()
            halo_copy(v, k, 0).wait_recv()

    def pack(v):
        def step(i, carry):
            low, high = carry
            x = i + 1
            for y in range(wide):
                tile = pads[v, x, y].astype(jnp.float32)
                here = lane == x * wide + y
                high = jnp.where(here, tile[:, nz - 1:nz], high)
                low = jnp.where(here, tile[:, 0:1], low)
            return low, high
        low, high = lax.fori_loop(0, nx, step, (zero, zero))
        edge_out[v, 0] = high.astype(jnp.bfloat16)
        edge_out[v, 1] = low.astype(jnp.bfloat16)

    def turned(tile, by):
        by = by % nz
        return pltpu.roll(tile, by, 1) if by else tile

    def unpack(v, shifted):
        for x in range(nx + 2):
            for side in range(2):
                if x == 0:
                    tile, at = edge_x[v, 0, side], nx * wide
                elif x == nx + 1:
                    tile, at = edge_x[v, 1, side], wide
                else:
                    tile, at = edge_in[v, side], x * wide
                bases[x, side] = turned(tile.astype(jnp.float32), -at - side)

        def step(x, carry):
            for y in range(wide):
                row = x * wide + y
                own = pads[v, x, y]
                tile = own.astype(jnp.float32)
                low = turned(bases[x, 0], -y)
                high = turned(bases[x, 1], -y)
                shifted[row, 0:chan] = jnp.where(
                    lane == 0, low, turned(tile, 1)).astype(jnp.bfloat16)
                shifted[row, chan:2 * chan] = own
                shifted[row, 2 * chan:] = jnp.where(
                    lane == nz - 1, high, turned(tile, -1)).astype(jnp.bfloat16)
            return carry
        lax.fori_loop(0, nx + 2, step, 0)

    def halo_rest(todo):
        for v, _ in todo:
            halo_wait(v, 1)
            halo_start(v, 3)
            halo_start(v, 4)
            pack(v)
            halo_start(v, 2)
        for v, _ in todo:
            halo_wait(v, 2)
            halo_start(v, 5)
        for v, shifted in todo:
            for k in (0, 3, 4, 5):
                halo_wait(v, k)
            unpack(v, shifted)

    def stacked(shifted, x, y):
        parts = []
        for tx in range(3):
            for ty in range(3):
                row = (x + tx) * wide + y + ty
                parts.append(jnp.concatenate([shifted[row], shifted[row + 1]], axis=1))
        return jnp.concatenate(parts, axis=0)

    def place(i):
        return i // half, (i % half) * 2

    def row_loop(body, init):
        def step(i, carry):
            x, y = i // (ny // 4), (i % (ny // 4)) * 4
            for u in range(4):
                carry = body(x, y + u, carry)
            return carry
        return lax.fori_loop(0, nx * (ny // 4), step, init)

    def total(value):
        return jnp.sum(value, axis=1, keepdims=True)

    def tile_of(values):
        tile = zero
        for at, value in enumerate(values):
            tile = jnp.where(lane == at, value, tile)
        return tile

    def all_sum(slots, k, send, recv):
        def copy(at, to, frm):
            return pltpu.make_async_remote_copy(
                src_ref=slots.at[at], dst_ref=slots.at[at], send_sem=send.at[to],
                recv_sem=recv.at[at], device_id=where(k, to), device_id_type=MESH)

        def start():
            for to, frm in peers(k):
                copy(rank[k], to, frm).start()

        def finish():
            for to, frm in peers(k):
                copy(rank[k], to, frm).wait_send()
                copy(frm, to, frm).wait_recv()
        return start, finish

    def reduce_stats(j, tile):
        for k in range(2):
            slots = stat.at[j, k]
            slots[rank[k]] = tile
            start, finish = all_sum(slots, k, sum_send.at[j, k], sum_recv.at[j, k])
            start()
            finish()
            tile = slots[0]
            for r in range(1, counts[k]):
                tile = tile + slots[r]
        return tile

    def weight_start(j, k, value):
        slots = wbuf.at[j, k]
        slots[rank[k]] = value.astype(jnp.bfloat16)
        all_sum(slots, k, w_send.at[j, k], w_recv.at[j, k])[0]()

    def weight_finish(j, k):
        slots = wbuf.at[j, k]
        all_sum(slots, k, w_send.at[j, k], w_recv.at[j, k])[1]()
        value = slots[0].astype(jnp.float32)
        for r in range(1, counts[k]):
            value = value + slots[r].astype(jnp.float32)
        return value

    def conv_stats(shift_one, shift_two, w, out_one, out_two):
        def step(i, carry):
            x, y = place(i)
            new = []
            for n, (shifted, out) in enumerate(((shift_one, out_one), (shift_two, out_two))):
                o = jnp.dot(w[...], stacked(shifted, x, y), preferred_element_type=jnp.float32)
                left, right = o[:, :nz], o[:, nz:]
                out[x, y] = left
                out[x, y + 1] = right
                new.append(carry[2 * n] + left + right)
                new.append(carry[2 * n + 1] + left * left + right * right)
            return tuple(new)
        return lax.fori_loop(0, nx * half, step, (zero,) * 4)

    def norm(tile, at):
        mean = tile[:, at:at + 1] / voxels
        var = tile[:, at + 1:at + 2] / voxels - mean * mean
        return jnp.broadcast_to(mean, zero.shape), jnp.broadcast_to(
            lax.rsqrt(var + EPSILON), zero.shape)

    def wgrad(v, shifted):
        wacc[...] = jnp.zeros(wacc.shape, jnp.float32)

        def step(i, carry):
            x, y = place(i)
            delta = jnp.concatenate([pads[v, x + 1, y + 1], pads[v, x + 1, y + 2]], axis=1)
            wacc[...] += lax.dot_general(
                delta, stacked(shifted, x, y), (((1,), (1,)), ((), ())),
                preferred_element_type=jnp.float32)
            return carry
        lax.fori_loop(0, nx * half, step, 0)

    def fill(x, y, carry):
        pads[0, x + 1, y + 1] = xa[x, y]
        pads[1, x + 1, y + 1] = xb[x, y]
        return carry
    row_loop(fill, 0)
    halo_start(0, 0)
    halo_start(0, 1)
    halo_start(1, 0)
    halo_start(1, 1)
    halo_rest(((0, shift_a), (1, shift_xb)))
    sums = conv_stats(shift_a, shift_xb, w1, c1a, c1b)
    tile = reduce_stats(0, tile_of([total(s) for s in sums]))
    mean_a, scale_a = norm(tile, 0)
    mean_one, scale_one = norm(tile, 2)
    gain_one = jnp.broadcast_to(g1[...], zero.shape)
    bias_one = jnp.broadcast_to(b1[...], zero.shape)
    gain_two = jnp.broadcast_to(g2[...], zero.shape)
    bias_two = jnp.broadcast_to(b2[...], zero.shape)

    def silu(z):
        return (z * jax.nn.sigmoid(z)).astype(jnp.bfloat16)

    def hidden(x, y, carry):
        za = gain_one * ((c1a[x, y] - mean_a) * scale_a) + bias_one
        pads[2, x + 1, y + 1] = silu(za)
        nb = (c1b[x, y] - mean_one) * scale_one
        c1b[x, y] = nb
        pads[3, x + 1, y + 1] = silu(gain_one * nb + bias_one)
        return carry
    row_loop(hidden, 0)
    halo_start(2, 0)
    halo_start(2, 1)
    halo_start(3, 0)
    halo_start(3, 1)
    halo_rest(((2, shift_a), (3, shift_hb)))
    sums = conv_stats(shift_a, shift_hb, w2, c2a, c2b)
    tile = reduce_stats(1, tile_of([total(s) for s in sums]))
    mean_a2, scale_a2 = norm(tile, 0)
    mean_two, scale_two = norm(tile, 2)

    def slope_two(x, y, carry):
        sd, sx = carry
        nb = (c2b[x, y] - mean_two) * scale_two
        c2b[x, y] = nb
        d = go[x, y].astype(jnp.float32) * slope_of(gain_two * nb + bias_two)
        d2[x, y] = d
        return sd + d, sx + d * nb
    sd, sx = row_loop(slope_two, (zero, zero))
    tile2 = reduce_stats(2, tile_of([total(sx), total(sd)]))
    sx2 = jnp.broadcast_to(tile2[:, 0:1] / voxels, zero.shape)
    sd2 = jnp.broadcast_to(tile2[:, 1:2] / voxels, zero.shape)

    def delta_two(x, y, carry):
        pads[4, x + 1, y + 1] = ((gain_two * scale_two) * (
            d2[x, y] - sd2 - c2b[x, y] * sx2)).astype(jnp.bfloat16)
        return carry
    row_loop(delta_two, 0)
    halo_start(4, 0)
    halo_start(4, 1)
    wgrad(4, shift_hb)

    def finish_a(x, y, carry):
        ya[x, y] = silu(gain_two * ((c2a[x, y] - mean_a2) * scale_a2) + bias_two)
        return carry
    row_loop(finish_a, 0)
    halo_rest(((4, shift_d),))
    weight_start(0, 0, wacc[...])

    def back(i, carry):
        x, y = place(i)
        sd, sx = carry
        o = jnp.dot(w2t[...], stacked(shift_d, x, y), preferred_element_type=jnp.float32)
        for u in range(2):
            nb = c1b[x, y + u]
            d = o[:, u * nz:(u + 1) * nz] * slope_of(gain_one * nb + bias_one)
            d1[x, y + u] = d
            sd, sx = sd + d, sx + d * nb
        return sd, sx
    sd, sx = lax.fori_loop(0, nx * half, back, (zero, zero))
    weight_start(0, 1, weight_finish(0, 0))
    tile1 = reduce_stats(3, tile_of([total(sx), total(sd)]))
    sx1 = jnp.broadcast_to(tile1[:, 0:1] / voxels, zero.shape)
    sd1 = jnp.broadcast_to(tile1[:, 1:2] / voxels, zero.shape)
    gnorm[...] = tile_of(
        [tile1[:, 0:1], tile1[:, 1:2], tile2[:, 0:1], tile2[:, 1:2]]) * factor

    def delta_one(x, y, carry):
        pads[5, x + 1, y + 1] = ((gain_one * scale_one) * (
            d1[x, y] - sd1 - c1b[x, y] * sx1)).astype(jnp.bfloat16)
        return carry
    row_loop(delta_one, 0)
    halo_start(5, 0)
    halo_start(5, 1)
    wgrad(5, shift_xb)
    halo_rest(((5, shift_d),))
    weight_start(1, 0, wacc[...])

    def last(i, carry):
        x, y = place(i)
        o = jnp.dot(w1t[...], stacked(shift_d, x, y), preferred_element_type=jnp.float32)
        for u in range(2):
            dxb[x, y + u] = o[:, u * nz:(u + 1) * nz].astype(jnp.bfloat16)
        return carry
    lax.fori_loop(0, nx * half, last, 0)
    weight_start(1, 1, weight_finish(1, 0))
    gw2[...] = weight_finish(0, 1) * factor
    gw1[...] = weight_finish(1, 1) * factor


def body(sizes, x_a, x_b, w_first, w_second, gain_first, bias_first, gain_second, bias_second,
         grad_out):
    chan, nx, ny, nz = x_a.shape
    voxels = float(nx * ny * nz * math.prod(sizes))
    taps = 27 * chan

    def rows(block):
        return block.transpose(1, 2, 0, 3)

    def matrix(w):
        return w.reshape(27, chan, chan).transpose(1, 0, 2).reshape(chan, taps)

    def flipped(w):
        return jnp.flip(w, (0, 1, 2)).transpose(0, 1, 2, 4, 3)

    def column(v):
        return v.reshape(chan, 1)

    most = max(sizes[0], sizes[1] * sizes[2])
    bf16, f32 = jnp.bfloat16, jnp.float32
    span = (nx + 2) * (ny + 2)
    grid = (nx, ny, chan, nz)
    vmem = pl.BlockSpec(memory_space=pltpu.VMEM)
    dma = pltpu.SemaphoreType.DMA
    y_a, dx_b, gw1, gw2, gnorm = pl.pallas_call(
        functools.partial(kernel, sizes, voxels),
        out_shape=(
            jax.ShapeDtypeStruct(grid, bf16),
            jax.ShapeDtypeStruct(grid, bf16),
            jax.ShapeDtypeStruct((chan, taps), f32),
            jax.ShapeDtypeStruct((chan, taps), f32),
            jax.ShapeDtypeStruct((chan, nz), f32),
        ),
        in_specs=[vmem] * 11,
        out_specs=[vmem] * 5,
        scratch_shapes=[
            pltpu.VMEM((6, nx + 2, ny + 2, chan, nz), bf16),
            pltpu.VMEM((6, 2, chan, nz), bf16),
            pltpu.VMEM((6, 2, chan, nz), bf16),
            pltpu.VMEM((6, 2, 2, chan, nz), bf16),
            pltpu.VMEM((nx + 2, 2, chan, nz), f32),
        ] + [pltpu.VMEM((span, 3 * chan, nz), bf16)] * 4
        + [pltpu.VMEM(grid, f32)] * 6
        + [
            pltpu.VMEM((4, 2, most, chan, nz), f32),
            pltpu.VMEM((2, 2, most, chan, taps), bf16),
            pltpu.VMEM((chan, taps), f32),
            dma((6, 6, 2)), dma((6, 6, 2)),
            dma((4, 2, most)), dma((4, 2, most)),
            dma((2, 2, most)), dma((2, 2, most)),
        ],
        compiler_params=pltpu.CompilerParams(
            collective_id=0, has_side_effects=True, vmem_limit_bytes=50 * 1024 * 1024),
    )(
        rows(x_a), rows(x_b), rows(grad_out),
        matrix(w_first), matrix(w_second), matrix(flipped(w_first)), matrix(flipped(w_second)),
        column(gain_first), column(bias_first), column(gain_second), column(bias_second),
    )

    def tensor(g):
        return g.reshape(chan, 27, chan).transpose(1, 0, 2).reshape(3, 3, 3, chan, chan)

    return (
        y_a.transpose(2, 0, 1, 3), dx_b.transpose(2, 0, 1, 3),
        tensor(gw1), tensor(gw2), gnorm[:, :4].T,
    )


def solution(mesh):
    sizes = tuple(mesh.shape[a] for a in AXES)
    split = P(None, *AXES)
    return jax.shard_map(
        functools.partial(body, sizes),
        mesh=mesh,
        in_specs=(split, split, P(), P(), P(), P(), P(), P(), split),
        out_specs=(split, split, P(), P(), P()),
        check_vma=False,
    )
```

profile of v0, /device:TPU:0, one launch (start us, length us, event | category | flops | bytes accessed | tf_op | source)
XLA Modules:
  0.0 120.2 jit_solution(17815939511130789728)
XLA Ops:
  0.6 0.0 copy-start.5
  0.6 0.6 copy-done.5
  1.3 0.0 copy-start.6
  1.3 0.1 copy.53.g1
  1.4 0.6 copy-done.6
  1.9 0.0 copy-start.7
  1.9 0.1 copy.54.b1
  2.0 0.6 copy-done.7
  2.6 0.0 copy-start.8
  2.6 0.1 copy.55.g2
  2.7 0.6 copy-done.8
  3.3 0.1 copy.56.b2
  3.3 0.9 rev.7
  4.3 0.4 copy.51
  4.7 0.0 copy-start
  4.7 0.2 reshape.63.w1t
  5.0 0.7 copy-done
  5.7 0.4 copy.52
  6.1 0.0 copy-start.2
  6.1 0.2 reshape.65.w2t
  6.4 0.7 copy-done.2
  7.1 0.1 copy.69
  7.2 0.1 copy.67
  7.3 0.0 copy-start.1
  7.3 0.2 reshape.61.w2
  7.6 0.7 copy-done.1
  8.2 0.0 copy-start.4
  8.2 0.1 copy.68
  8.3 0.0 copy-start.3
  8.3 0.2 reshape.59.w1
  8.6 0.6 copy-done.4
  9.2 0.1 copy-done.3
  9.3 0.2 copy_bitcast_fusion.2
  9.5 106.0 %shard_map.128 = (bf16[2,16,32,128]{3,2,1,0:T(8,128)(2,1)S(1)}, bf16[2,16,32,128]{3,2,1,0:T(8,128)(2,1)S(1)}, f32[32,864]{1,0:T(8,128)S(1)}, f32[32,864]{1,0:T(8,128)S(1)}, f32[32,128]{1,0:T(8,128)S(1)}) custom-call(bf16[2,16,32,128]{3,2,1,0:T(8,128)(2,1)S(1)} %bitcast.35, bf16[2,16,32,128]{3,2,1,0:T(8,128)(2,1)S(1)} %get-tuple-element.31.xb, ...), custom_call_target="tpu_custom_call" | custom-call | tf_op jit(solution)/shard_map/pallas_call | solution.py:407
  115.5 0.8 copy.59
  116.3 0.8 copy.60
  117.1 0.7 copy.61
  117.8 0.2 reshape.70
  118.0 1.0 copy.57
  119.0 0.2 reshape.72
  119.2 1.0 copy.58
  (2 shorter events, 0.0 us)
Async XLA Ops:
  0.6 0.7 copy-start.5
  1.3 0.7 copy-start.6
  1.9 0.7 copy-start.7
  2.6 0.7 copy-start.8
  4.7 0.9 copy-start
  6.1 1.0 copy-start.2
  7.3 0.9 copy-start.1
  8.2 0.9 copy-start.4
  8.3 1.0 copy-start.3
where the time goes:
time: 121 us; the launch traced here: 120 us
  Pallas kernels  106 us (88%)
  local copies, waits for them, and re-layouts  13.4 us (11%)
    pallas_call x1, Pallas kernels, body(): pl.pallas_call(functools.partial(kernel, sizes, voxels), out_shape=(jax.S...  106 us
    unnamed x22, local copies, waits for them, and re-layouts  7.51 us

commit v1 on v0

v1 whole, which is shorter than its diff:
```python
import functools
import math

import jax
import jax.numpy as jnp
from jax import lax
from jax.experimental import pallas as pl
from jax.experimental.pallas import tpu as pltpu
from jax.sharding import PartitionSpec as P

EPSILON = 1e-05
AXES = ("gx", "gy", "gz")
MESH = pl.DeviceIdType.MESH
XB, XA, GO, C1B, C1A, C2B, E1 = range(7)
D2, D1 = 7, 8
OFFSETS = [(a, b, c) for a in (-1, 0, 1) for b in (-1, 0, 1) for c in (-1, 0, 1)
           if (a, b, c) != (0, 0, 0)]
GROUP = 4
DEEP = 8


def slope_of(z):
    s = jax.nn.sigmoid(z)
    return s * (1.0 + z * (1.0 - s))


def code(offset):
    a, b, c = offset
    return (a + 1) * 9 + (b + 1) * 3 + c + 1


def minus(offset):
    return tuple(-o for o in offset)


def kernel(
    sizes, voxels, units,
    xa, xb, go, w1, w2, g1, b1, g2, b2,
    ya, dxb, gw1, gw2, gnorm,
    raw, wraw, gains, tall, mats, pads, edge_out, edge_in, cols,
    shift_xb, shift_a, shift_hb, shift_d,
    f1b, f1a, f2b, fd2, fd1, c2a, e1, slots, wsum, wunit, wslot, wfull,
    load_sem, halo_send, halo_recv, sum_send, sum_recv, w_send, w_recv,
):
    chan, nx, ny, nz = raw.shape[1:]
    wide = ny + 2
    own = nx * ny
    pitch = tall.shape[0] // chan
    count = math.prod(sizes)
    local = float(own * nz)
    factor = 1.0 / math.sqrt(voxels)
    me = [lax.axis_index(a) for a in AXES]
    rank = (me[0] * sizes[1] + me[1]) * sizes[2] + me[2]
    lane = lax.broadcasted_iota(jnp.int32, (chan, nz), 1)
    chan_of = lax.broadcasted_iota(jnp.int32, (chan, nz), 0)
    zero = jnp.zeros((chan, nz), jnp.float32)
    bf16, f32 = jnp.bfloat16, jnp.float32

    others = [(a, b, c) for a in range(sizes[0]) for b in range(sizes[1])
              for c in range(sizes[2])][1:]

    def at_offset(offset):
        return [lax.rem(m + o, s) for m, o, s in zip(me, offset, sizes)]

    def ids(place):
        return dict(zip(AXES, place))

    barrier = pltpu.get_barrier_semaphore()
    for offset in others:
        pl.semaphore_signal(
            barrier, inc=1, device_id=ids(at_offset(offset)), device_id_type=MESH)

    loads = []
    for at, (src, dst) in enumerate((
            (xb, raw.at[0]), (w1, wraw.at[0]), (xa, raw.at[1]), (go, raw.at[2]),
            (w2, wraw.at[1]), (g1, gains.at[0]), (b1, gains.at[1]), (g2, gains.at[2]),
            (b2, gains.at[3]))):
        copy = pltpu.make_async_copy(src, dst, load_sem.at[at])
        copy.start()
        loads.append(copy)

    inside = []
    for k in range(3):
        inside.append({-1: me[k] > 0, 0: None, 1: me[k] < sizes[k] - 1})

    def reaches(offset):
        known = [inside[k][o] for k, o in enumerate(offset) if o]
        flag = known[0]
        for more in known[1:]:
            flag = jnp.logical_and(flag, more)
        return flag

    def halo_copies(v, offset, centred):
        to = ids([me[k] + o for k, o in enumerate(offset)])

        def remote(src, dst, m):
            return pltpu.make_async_remote_copy(
                src_ref=src, dst_ref=dst, send_sem=halo_send.at[v, m],
                recv_sem=halo_recv.at[v, m], device_id=to, device_id_type=MESH)

        found = []
        if centred or offset[2]:
            found.append(remote(edge_out.at[v], edge_in.at[v, code(offset)], code(offset)))
        if not offset[2]:
            def cut(o, n):
                if o == 0:
                    return pl.ds(1, n), pl.ds(1, n)
                return (n, 0) if o > 0 else (1, n + 1)
            (sx, dx), (sy, dy) = cut(offset[0], nx), cut(offset[1], ny)
            m = 27 + (offset[0] + 1) * 3 + offset[1] + 1
            found.append(remote(pads.at[v, sx, sy], pads.at[v, dx, dy], m))
        return found

    order = sorted(OFFSETS, key=lambda o: (o[2] == 0, o[1] == 0 and o[2] == 0))

    def halo_start(v, centred=False):
        for offset in order:
            @pl.when(reaches(offset))
            def _(offset=offset):
                for copy in halo_copies(v, offset, centred):
                    copy.start()

    def halo_wait(v, centred=False):
        for offset in order:
            @pl.when(reaches(offset))
            def _(offset=offset):
                for copy in halo_copies(v, offset, centred):
                    copy.wait_send()
                for copy in halo_copies(v, minus(offset), centred):
                    copy.wait_recv()

    def total(value):
        return jnp.sum(value, axis=1, keepdims=True)

    def turned(tile, by):
        return pltpu.roll(tile, by, 1)

    def emit(v, tile_of, centre=None):
        def step(x, edge):
            for y in range(ny):
                tile = tile_of(x, y)
                if centre is not None:
                    tile = tile - centre
                pads[v, x + 1, y + 1] = tile.astype(bf16)
                r = x * ny + y
                edge = jnp.where(lane == r, tile[:, 0:1], edge)
                edge = jnp.where(lane == own + r, tile[:, nz - 1:nz], edge)
            return edge
        edge = lax.fori_loop(0, nx, step, zero if centre is None else centre)
        edge_out[v] = edge.astype(bf16)

    def edge_tile(v, near, centred):
        tile = edge_in[v, code(minus(near))].astype(f32)
        return tile + tile[:, nz - 1:nz] if centred else tile

    def collect_columns(v, centred=False):
        for side in range(2):
            dz = 2 * side - 1
            first = 0 if side else own
            for dx in (-1, 0, 1):
                left, mid, right = [edge_tile(v, (dx, dy, dz), centred) for dy in (-1, 0, 1)]
                for x in ((0,), range(1, nx + 1), (nx + 1,))[dx + 1]:
                    base = first + (nx - 1, x - 1, 0)[dx + 1] * ny
                    tile = turned(mid, (1 - base) % nz)
                    tile = jnp.where(lane == 0, turned(left, (1 - base - ny) % nz), tile)
                    tile = jnp.where(lane == ny + 1, turned(right, (ny + 1 - base) % nz), tile)
                    cols[v, x, side] = tile

    def halo_rows(fn):
        def step(y, carry):
            fn(0, y, (-1, 0, 0))
            fn(nx + 1, y, (1, 0, 0))
            return carry
        lax.fori_loop(1, ny + 1, step, 0)
        for y, dy in ((0, -1), (ny + 1, 1)):
            for x in range(nx + 2):
                fn(x, y, (-1 if x == 0 else 1 if x == nx + 1 else 0, dy, 0))

    def collect_centred(v, full):
        collect_columns(v, True)
        centres = {}
        for dx in (-1, 0, 1):
            for dy in (-1, 0, 1):
                if dx or dy:
                    tile = edge_in[v, code((-dx, -dy, 0))].astype(f32)
                    centres[dx, dy, 0] = jnp.broadcast_to(tile[:, nz - 1:nz], zero.shape)

        def fn(x, y, near):
            full[x, y] = pads[v, x, y].astype(f32) + centres[near]
        halo_rows(fn)

    def build(tile_of, shifted, turn):
        low_y = jnp.where(me[1] > 0, 0, 1)
        high_y = jnp.where(me[1] < sizes[1] - 1, wide, wide - 1)

        def step(x, carry):
            x_ok = jnp.logical_and(
                jnp.logical_or(x > 0, me[0] > 0),
                jnp.logical_or(x < nx + 1, me[0] < sizes[0] - 1))
            ok = {1: x_ok, 0: jnp.logical_and(x_ok, me[1] > 0),
                  2: jnp.logical_and(x_ok, me[1] < sizes[1] - 1)}
            some = {k: jnp.where(f, nz, 0) for k, f in ok.items()}
            sides = []
            for side, flag in ((0, me[2] > 0), (1, me[2] < sizes[2] - 1)):
                last = jnp.where(jnp.logical_and(x_ok, flag), high_y, 0)
                keep = jnp.logical_and(lane >= low_y, lane < last)
                sides.append(jnp.where(keep, tile_of(x, wide + side), 0.0))
            for y in range(wide):
                limit = some[0 if y == 0 else 2 if y == wide - 1 else 1]
                tile = jnp.where(lane < limit, tile_of(x, y), 0.0)
                low = jnp.where(lane == 0, turned(sides[0], (nz - y) % nz), turned(tile, 1))
                high = jnp.where(
                    lane == nz - 1, turned(sides[1], nz - 1 - y), turned(tile, nz - 1))
                row = x * wide + y
                shifted[row, 0:chan] = (high if turn else low).astype(bf16)
                shifted[row, chan:2 * chan] = tile.astype(bf16)
                shifted[row, 2 * chan:] = (low if turn else high).astype(bf16)
            return carry
        lax.fori_loop(0, nx + 2, step, 0)

    def at(full, v):
        def tile_of(x, y):
            return cols[v, x, y - wide] if isinstance(y, int) and y >= wide else full[x, y]
        return tile_of

    def at_pads(v):
        def tile_of(x, y):
            if isinstance(y, int) and y >= wide:
                return cols[v, x, y - wide]
            return pads[v, x, y].astype(f32)
        return tile_of

    def stacked(shifted, x, y, n, turn=False):
        parts = []
        for tx in range(3):
            for ty in range(3):
                row = (x + (2 - tx if turn else tx)) * wide + y + (2 - ty if turn else ty)
                parts.append(jnp.concatenate([shifted[row + u] for u in range(n)], axis=1))
        return jnp.concatenate(parts, axis=0)

    def conv_rows(shifted, w, turn, finish, init):
        def step(i, carry):
            x, y0 = i // (ny // DEEP), (i % (ny // DEEP)) * DEEP
            for p in range(0, DEEP, GROUP):
                o = jnp.dot(w, stacked(shifted, x, y0 + p, GROUP, turn),
                            preferred_element_type=f32)
                for u in range(GROUP):
                    carry = finish(x, y0 + p + u, o[:, u * nz:(u + 1) * nz], carry)
            return carry
        return lax.fori_loop(0, nx * (ny // DEEP), step, init)

    def conv_stats(shifted, w, full, shift):
        def finish(x, y, o, carry):
            full[x + shift, y + shift] = o
            return carry[0] + o, carry[1] + o * o
        return conv_rows(shifted, w, False, finish, (zero, zero))

    def row_of(values):
        tile = zero
        for k, value in enumerate(values):
            tile = jnp.where(lane == k * chan + chan_of, value, tile)
        return jnp.sum(tile, axis=0, keepdims=True)

    def column(row, k):
        return total(jnp.where(lane == k * chan + chan_of, row, 0.0))

    def spread(value):
        return jnp.broadcast_to(value, zero.shape)

    def all_start(buf, value, j, send, recv):
        buf[rank] = value
        for offset in others:
            to = at_offset(offset)
            pltpu.make_async_remote_copy(
                src_ref=buf.at[rank], dst_ref=buf.at[rank], send_sem=send.at[j],
                recv_sem=recv.at[j], device_id=ids(to), device_id_type=MESH).start()

    def wait_bytes(buf, sem):
        some = buf.at[pl.ds(0, count - 1)]
        pltpu.make_async_copy(some, some, sem).wait()

    def tree(values):
        while len(values) > 1:
            values = [values[i] + values[i + 1] if i + 1 < len(values) else values[i]
                      for i in range(0, len(values), 2)]
        return values[0]

    def sums_start(j, values):
        all_start(slots.at[j], row_of([total(v) for v in values]), j, sum_send, sum_recv)

    def sums_finish(j):
        wait_bytes(slots.at[j], sum_recv.at[j])
        wait_bytes(slots.at[j], sum_send.at[j])
        return tree([slots[j, r] for r in range(count)])

    def norm(row):
        mean = column(row, 0) / voxels
        var = column(row, 1) / voxels - mean * mean
        return spread(mean), spread(lax.rsqrt(var + EPSILON))

    def centre_of(sums):
        return spread(total(sums[0]) / local).astype(bf16).astype(f32)

    def weights_start(j, value):
        tiles = value.shape[1] // nz
        for u in range(tiles * (chan // 8)):
            r, t = u // tiles, u % tiles
            wunit[j, u // units, pl.ds((u % units) * 8, 8)] = value[
                r * 8:r * 8 + 8, t * nz:(t + 1) * nz]
        wslot[j, rank] = wunit[j, rank]
        for offset in others:
            to = at_offset(offset)
            r = (to[0] * sizes[1] + to[1]) * sizes[2] + to[2]
            pltpu.make_async_remote_copy(
                src_ref=wunit.at[j, r], dst_ref=wslot.at[j, rank], send_sem=w_send.at[j],
                recv_sem=w_recv.at[j], device_id=ids(to), device_id_type=MESH).start()

    def weights_share(j):
        wait_bytes(wslot.at[j], w_recv.at[j])
        wait_bytes(wslot.at[j], w_send.at[j])
        value = tree([wslot[j, r] for r in range(count)]) * factor
        all_start(wfull.at[j], value, 2 + j, w_send, w_recv)

    def weights_finish(j, out):
        wait_bytes(wfull.at[j], w_recv.at[2 + j])
        wait_bytes(wfull.at[j], w_send.at[2 + j])
        tiles = wsum.shape[1] // nz
        for u in range(tiles * (chan // 8)):
            r, t = u // tiles, u % tiles
            piece = wfull[j, u // units, pl.ds((u % units) * 8, 8)]
            for k in range(nz // chan):
                tap = t * (nz // chan) + k
                if tap < 27:
                    out[tap, pl.ds(r * 8, 8)] = piece[:, k * chan:(k + 1) * chan]

    def wgrad(shifted_d, shifted):
        wsum[...] = jnp.zeros(wsum.shape, f32)

        def step(i, carry):
            x, y = i // (ny // DEEP), (i % (ny // DEEP)) * DEEP
            row = (x + 1) * wide + y + 1
            delta = jnp.concatenate(
                [shifted_d[row + u, chan:2 * chan] for u in range(DEEP)], axis=1)
            wsum[:, 0:27 * chan] += lax.dot_general(
                delta, stacked(shifted, x, y, DEEP), (((1,), (1,)), ((), ())),
                preferred_element_type=f32)
            return carry
        lax.fori_loop(0, nx * (ny // DEEP), step, 0)
        return wsum[...]

    def take(k):
        def step(c, carry):
            at_row = pl.multiple_of(c * pitch, 8)
            for x in range(nx):
                tall[pl.ds(at_row + x * ny, ny)] = raw[k, c, x].astype(f32)
            return carry
        lax.fori_loop(0, chan, step, 0, unroll=4)

        def tile_of(x, y):
            return tall[pl.ds(x * ny + y, chan, stride=pitch)]
        return tile_of

    def give(out):
        def step(c, carry):
            at_row = pl.multiple_of(c * pitch, 8)
            for x in range(nx):
                out[c, x] = tall[pl.ds(at_row + x * ny, ny)].astype(bf16)
            return carry
        lax.fori_loop(0, chan, step, 0, unroll=4)

    def put_row(x, y, tile):
        tall[pl.ds(x * ny + y, chan, stride=pitch)] = tile

    def prepare(k):
        taps = [wraw[k, t].astype(f32) for t in range(27)]
        mats[2 * k] = jnp.concatenate(taps, axis=1).astype(bf16)
        mats[2 * k + 1] = jnp.concatenate(taps, axis=0).T.astype(bf16)

    loads[0].wait()
    emit(XB, take(0))
    pl.semaphore_wait(barrier, count - 1)
    halo_start(XB)
    loads[2].wait()
    emit(XA, take(1))
    halo_start(XA)
    loads[3].wait()
    emit(GO, take(2))
    halo_start(GO)
    loads[1].wait()
    prepare(0)
    loads[4].wait()
    prepare(1)
    for k in range(5, 9):
        loads[k].wait()

    def gain(k):
        value = spread(jnp.concatenate([gains[k]] * (nz // chan), axis=1))
        return spread(column(value, 0))
    gain_one, bias_one, gain_two, bias_two = [gain(k) for k in range(4)]

    halo_wait(XB)
    collect_columns(XB)
    build(at_pads(XB), shift_xb, False)
    sums = conv_stats(shift_xb, mats[0], f1b, 1)
    sums_start(0, sums)
    emit(C1B, lambda x, y: f1b[x + 1, y + 1], centre_of(sums))
    halo_start(C1B, True)

    halo_wait(XA)
    collect_columns(XA)
    build(at_pads(XA), shift_a, False)
    sums = conv_stats(shift_a, mats[0], f1a, 1)
    sums_start(1, sums)
    emit(C1A, lambda x, y: f1a[x + 1, y + 1], centre_of(sums))
    halo_start(C1A, True)

    def silu(z):
        return z * jax.nn.sigmoid(z)

    halo_wait(C1B, True)
    collect_centred(C1B, f1b)
    mean_one, scale_one = norm(sums_finish(0))
    steep_one = gain_one * scale_one
    tile_1b = at(f1b, C1B)

    def z_one(x, y):
        return (tile_1b(x, y) - mean_one) * steep_one + bias_one
    build(lambda x, y: silu(z_one(x, y)), shift_hb, False)
    sums = conv_stats(shift_hb, mats[2], f2b, 1)
    sums_start(2, sums)
    emit(C2B, lambda x, y: f2b[x + 1, y + 1], centre_of(sums))
    halo_start(C2B, True)

    halo_wait(C1A, True)
    collect_centred(C1A, f1a)
    mean_a, scale_a = norm(sums_finish(1))
    steep_a = gain_one * scale_a
    tile_1a = at(f1a, C1A)
    build(lambda x, y: silu((tile_1a(x, y) - mean_a) * steep_a + bias_one), shift_a, False)
    sums_start(3, conv_stats(shift_a, mats[2], c2a, 0))

    halo_wait(GO)
    collect_columns(GO)
    halo_wait(C2B, True)
    collect_centred(C2B, f2b)
    mean_two, scale_two = norm(sums_finish(2))
    steep_two = gain_two * scale_two
    tile_2b = at(f2b, C2B)
    tile_go = at_pads(GO)

    def d_two(x, y):
        return tile_go(x, y) * slope_of((tile_2b(x, y) - mean_two) * steep_two + bias_two)

    def own_two(x, carry):
        sd, sx = carry
        for y in range(1, ny + 1):
            d = d_two(x, y)
            fd2[x, y] = d
            sd, sx = sd + d, sx + d * (tile_2b(x, y) - mean_two)
        return sd, sx
    sd, sx = lax.fori_loop(1, nx + 1, own_two, (zero, zero))
    sums_start(4, (sx * scale_two, sd))

    def halo_two(x, y, near):
        fd2[x, y] = d_two(x, y)
    halo_rows(halo_two)
    for x in range(nx + 2):
        for side in range(2):
            cols[D2, x, side] = d_two(x, wide + side)

    mean_a2, scale_a2 = norm(sums_finish(3))
    steep_a2 = gain_two * scale_a2

    def finish_a(x, carry):
        for y in range(ny):
            put_row(x, y, silu((c2a[x, y] - mean_a2) * steep_a2 + bias_two))
        return carry
    lax.fori_loop(0, nx, finish_a, 0)
    give(ya)

    row_two = sums_finish(4)
    sx2 = spread(column(row_two, 0) / voxels) * scale_two
    sd2 = spread(column(row_two, 1) / voxels)
    tile_d2 = at(fd2, D2)
    build(lambda x, y: steep_two * (tile_d2(x, y) - sd2 - (tile_2b(x, y) - mean_two) * sx2),
          shift_d, True)

    def back(x, y, o, carry):
        sd, sx = carry
        e1[x, y] = o
        d = o * slope_of(z_one(x + 1, y + 1))
        fd1[x + 1, y + 1] = d
        return sd + d, sx + d * (tile_1b(x + 1, y + 1) - mean_one)
    sd, sx = conv_rows(shift_d, mats[3], True, back, (zero, zero))
    sums_start(5, (sx * scale_one, sd))
    emit(E1, lambda x, y: e1[x, y])
    halo_start(E1)
    weights_start(0, wgrad(shift_d, shift_hb))

    halo_wait(E1)
    collect_columns(E1)

    def halo_one(x, y, near):
        fd1[x, y] = pads[E1, x, y].astype(f32) * slope_of(z_one(x, y))
    halo_rows(halo_one)
    for x in range(nx + 2):
        for side in range(2):
            cols[D1, x, side] = cols[E1, x, side] * slope_of(z_one(x, wide + side))

    row_one = sums_finish(5)
    sx1 = spread(column(row_one, 0) / voxels) * scale_one
    sd1 = spread(column(row_one, 1) / voxels)
    tile_d1 = at(fd1, D1)
    build(lambda x, y: steep_one * (tile_d1(x, y) - sd1 - (tile_1b(x, y) - mean_one) * sx1),
          shift_d, True)
    weights_start(1, wgrad(shift_d, shift_xb))
    weights_share(0)

    def last(x, y, o, carry):
        put_row(x, y, o)
        return carry
    conv_rows(shift_d, mats[1], True, last, 0)
    give(dxb)
    for k, row in enumerate((row_one, row_two)):
        for j in range(2):
            gnorm[2 * k + j:2 * k + j + 1, :] = row[:, j * chan:(j + 1) * chan] * factor
    weights_finish(0, gw2)
    weights_share(1)
    weights_finish(1, gw1)


def deliver(*refs):
    sem = refs[-1]
    half = (len(refs) - 1) // 2
    copies = [pltpu.make_async_copy(src, dst, sem.at[k])
              for k, (src, dst) in enumerate(zip(refs[:half], refs[half:-1]))]
    for copy in copies:
        copy.start()
    for copy in copies:
        copy.wait()


def body(sizes, x_a, x_b, w_first, w_second, gain_first, bias_first, gain_second, bias_second,
         grad_out):
    chan, nx, ny, nz = x_a.shape
    count = math.prod(sizes)
    voxels = float(nx * ny * nz * count)
    taps = 27 * chan
    bf16, f32 = jnp.bfloat16, jnp.float32
    tiles = -(-taps // nz)
    units = -(-tiles * (chan // 8) // count)
    full = (nx + 2, ny + 2, chan, nz)
    span = (nx + 2) * (ny + 2)
    grid = (nx, ny, chan, nz)
    vmem = pl.BlockSpec(memory_space=pltpu.VMEM)
    hbm = pl.BlockSpec(memory_space=pl.ANY)
    dma = pltpu.SemaphoreType.DMA
    shapes = (
        jax.ShapeDtypeStruct(x_a.shape, bf16),
        jax.ShapeDtypeStruct(x_a.shape, bf16),
        jax.ShapeDtypeStruct((27, chan, chan), f32),
        jax.ShapeDtypeStruct((27, chan, chan), f32),
        jax.ShapeDtypeStruct((4, chan), f32),
    )
    results = pl.pallas_call(
        functools.partial(kernel, sizes, voxels, units),
        out_shape=shapes,
        in_specs=[hbm] * 9,
        out_specs=[vmem] * 5,
        scratch_shapes=[
            pltpu.VMEM((3, chan, nx, ny, nz), bf16),
            pltpu.VMEM((2, 27, chan, chan), bf16),
            pltpu.VMEM((4, 1, chan), f32),
            pltpu.VMEM((chan * (nx * ny + 8), nz), f32),
            pltpu.VMEM((4, chan, taps), bf16),
            pltpu.VMEM((7,) + full, bf16),
            pltpu.VMEM((7, chan, nz), bf16),
            pltpu.VMEM((7, 27, chan, nz), bf16),
            pltpu.VMEM((9, nx + 2, 2, chan, nz), f32),
        ] + [pltpu.VMEM((span, 3 * chan, nz), bf16)] * 4
        + [pltpu.VMEM(full, f32)] * 5
        + [pltpu.VMEM(grid, f32)] * 2
        + [
            pltpu.VMEM((6, count, 1, nz), f32),
            pltpu.VMEM((chan, tiles * nz), f32),
            pltpu.VMEM((2, count, 8 * units, nz), f32),
            pltpu.VMEM((2, count, 8 * units, nz), f32),
            pltpu.VMEM((2, count, 8 * units, nz), f32),
            dma((9,)),
            dma((7, 36)), dma((7, 36)),
            dma((6,)), dma((6,)),
            dma((4,)), dma((4,)),
        ],
        compiler_params=pltpu.CompilerParams(
            collective_id=0, has_side_effects=True, vmem_limit_bytes=56 * 1024 * 1024),
    )(
        x_a, x_b, grad_out,
        w_first.reshape(27, chan, chan), w_second.reshape(27, chan, chan),
        gain_first.reshape(1, chan), bias_first.reshape(1, chan),
        gain_second.reshape(1, chan), bias_second.reshape(1, chan),
    )
    y_a, dx_b, gw1, gw2, gnorm = pl.pallas_call(
        deliver,
        out_shape=shapes,
        in_specs=[vmem] * 5,
        out_specs=[hbm] * 5,
        scratch_shapes=[dma((5,))],
    )(*results)
    cube = (3, 3, 3, chan, chan)
    return y_a, dx_b, gw1.reshape(cube), gw2.reshape(cube), gnorm


def solution(mesh):
    sizes = tuple(mesh.shape[a] for a in AXES)
    split = P(None, *AXES)
    return jax.shard_map(
        functools.partial(body, sizes),
        mesh=mesh,
        in_specs=(split, split, P(), P(), P(), P(), P(), P(), split),
        out_specs=(split, split, P(), P(), P()),
        check_vma=False,
    )
```

time: 121 us -> 74.2 us (0.61)
  Pallas kernels: 106 us -> 73.4 us
  local copies, waits for them, and re-layouts: 13.4 us -> 0 us
    pallas_call x1 -> x2, Pallas kernels: 106 us -> 73.4 us  [the longest x1 70.9 us: body(): pl.pallas_call(functools.partial(kernel, sizes, voxels, units), out_shape...]
    unnamed x22 -> x0, local copies, waits for them, and re-layouts: 7.51 us -> none
    reshape x14 -> x0, local copies, waits for them, and re-layouts: 2.72 us -> none  [the longest x8 2.02 us: matrix(): return w.reshape(27, chan, chan).transpose(1, 0, 2).reshape(chan, taps)]
    transpose x4 -> x0, local copies, waits for them, and re-layouts: 2.26 us -> none  [the longest x2 2.05 us: tensor(): g.reshape(chan, 27, chan).transpose(1, 0, 2).reshape(3, 3, 3, chan, chan)]
where the time goes in v1:
time: 74.2 us; the launch traced here: 74 us
  Pallas kernels  73.4 us (99%)
    pallas_call x1, Pallas kernels, body(): pl.pallas_call(functools.partial(kernel, sizes, voxels, units), out_shape...  70.9 us
    pallas_call x1, Pallas kernels, body(): pl.pallas_call(deliver, out_shape=shapes, in_specs=[vmem] * 5, out_specs=...  2.44 us

profile of v1, /device:TPU:0, one launch (start us, length us, event | category | flops | bytes accessed | tf_op | source)
XLA Modules:
  0.0 74.0 jit_solution(16605846446686486049)
XLA Ops:
  0.6 70.9 %shard_map.128 = (bf16[32,2,16,128]{3,2,1,0:T(8,128)(2,1)}, bf16[32,2,16,128]{3,2,1,0:T(8,128)(2,1)}, f32[27,32,32]{2,1,0:T(8,128)}, f32[27,32,32]{2,1,0:T(8,128)}, f32[4,32]{1,0:T(4,128)}) custom-call(bf16[32,2,16,128]{3,2,1,0:T(8,128)(2,1)} %xa.1, bf16[32,2,16,128]{3,2,1,0:T(8,128)(2,1)} %xb.1, bf16[32,2,16,128]{3,2,1,0:T(8,128)(2,1)} %go.1, ...), custom_call_target="tpu_custom_call" | custom-call | tf_op jit(solution)/shard_map/pallas_call | solution.py:565
  71.6 2.4 %shard_map.129 = (bf16[32,2,16,128]{3,2,1,0:T(8,128)(2,1)}, bf16[32,2,16,128]{3,2,1,0:T(8,128)(2,1)}, f32[27,32,32]{2,1,0:T(8,128)}, f32[27,32,32]{2,1,0:T(8,128)}, f32[4,32]{1,0:T(4,128)}) custom-call(bf16[32,2,16,128]{3,2,1,0:T(8,128)(2,1)} %get-tuple-element.15.refs_0_, bf16[32,2,16,128]{3,2,1,0:T(8,128)(2,1)} %get-tuple-element.16.refs_1_, ...), custom_call_target="tpu_custom_call" | custom-call | tf_op jit(solution)/shard_map/pallas_call | solution.py:602

commit v2 on v1

v2 whole, which is shorter than its diff:
```python
import functools
import math

import jax
import jax.numpy as jnp
from jax import lax
from jax.experimental import pallas as pl
from jax.experimental.pallas import tpu as pltpu
from jax.sharding import PartitionSpec as P

EPSILON = 1e-05
AXES = ("gx", "gy", "gz")
MESH = pl.DeviceIdType.MESH
XB, XA, GO, C1B, C1A, C2B, E1 = range(7)
D2, D1 = range(2)
OFFSETS = [(a, b, c) for a in (-1, 0, 1) for b in (-1, 0, 1) for c in (-1, 0, 1)
           if (a, b, c) != (0, 0, 0)]
DEEP = 4


def slope_of(z):
    s = jax.nn.sigmoid(z)
    return s * (1.0 + z * (1.0 - s))


def code(offset):
    a, b, c = offset
    return (a + 1) * 9 + (b + 1) * 3 + c + 1


def minus(offset):
    return tuple(-o for o in offset)


def kernel(
    sizes, voxels, units,
    xa, xb, go, w1, w2, g1, b1, g2, b2,
    ya, dxb, gw1, gw2, gnorm,
    raw, wraw, gains, tall, mats, pads, edge_out, edge_in, cols, dcols, offs,
    shift_xb, shift_a, shift_hb, shift_d,
    fd2, fd1, c1b, c1a, c2b, c2a, e1, d1h, slots, xsum, xfull, kcol, wsum,
    unit_h, slot_h, unit_f, slot_f, wfull,
    load_sem, halo_send, halo_recv, sum_send, sum_recv, w_send, w_recv,
):
    chan, nx, ny, nz = raw.shape[1:]
    wide = ny + 2
    own = nx * ny
    pitch = tall.shape[0] // chan
    count = math.prod(sizes)
    local = float(own * nz)
    factor = 1.0 / math.sqrt(voxels)
    tiles = wsum.shape[1] // nz
    me = [lax.axis_index(a) for a in AXES]

    def rank_of(place):
        return (place[0] * sizes[1] + place[1]) * sizes[2] + place[2]
    rank = rank_of(me)
    lane = lax.broadcasted_iota(jnp.int32, (chan, nz), 1)
    chan_of = lax.broadcasted_iota(jnp.int32, (chan, nz), 0)
    odd = lax.rem(lane, 2) == 1
    zero = jnp.zeros((chan, nz), jnp.float32)
    bf16, f32 = jnp.bfloat16, jnp.float32

    others = [(a, b, c) for a in range(sizes[0]) for b in range(sizes[1])
              for c in range(sizes[2])][1:]

    def at_offset(offset):
        return [lax.rem(m + o + s, s) for m, o, s in zip(me, offset, sizes)]

    def ids(place):
        return dict(zip(AXES, place))

    barrier = pltpu.get_barrier_semaphore()
    for offset in others:
        pl.semaphore_signal(
            barrier, inc=1, device_id=ids(at_offset(offset)), device_id_type=MESH)

    loads = []
    for at, (src, dst) in enumerate((
            (xb, raw.at[0]), (w1, wraw.at[0]), (xa, raw.at[1]), (go, raw.at[2]),
            (w2, wraw.at[1]), (g1, gains.at[0]), (b1, gains.at[1]), (g2, gains.at[2]),
            (b2, gains.at[3]))):
        copy = pltpu.make_async_copy(src, dst, load_sem.at[at])
        copy.start()
        loads.append(copy)

    inside = []
    for k in range(3):
        inside.append({-1: me[k] > 0, 0: None, 1: me[k] < sizes[k] - 1})

    def reaches(offset):
        known = [inside[k][o] for k, o in enumerate(offset) if o]
        flag = known[0]
        for more in known[1:]:
            flag = jnp.logical_and(flag, more)
        return flag

    def halo_copy(v, offset):
        to = ids([me[k] + o for k, o in enumerate(offset)])
        if offset[2]:
            src, dst = edge_out.at[v], edge_in.at[v, code(offset)]
        else:
            def cut(o, n):
                if o == 0:
                    return pl.ds(1, n), pl.ds(1, n)
                return (n, 0) if o > 0 else (1, n + 1)
            (sx, dx), (sy, dy) = cut(offset[0], nx), cut(offset[1], ny)
            src, dst = pads.at[v, sx, sy], pads.at[v, dx, dy]
        m = code(offset)
        return pltpu.make_async_remote_copy(
            src_ref=src, dst_ref=dst, send_sem=halo_send.at[v, m],
            recv_sem=halo_recv.at[v, m], device_id=to, device_id_type=MESH)

    order = sorted(OFFSETS, key=lambda o: (o[1] == 0 and o[2] == 0, o[0] != 0))
    sides = [o for o in order if o[0] == 0]
    faces = [o for o in order if o[0] != 0]

    def halo_start(v):
        for offset in order:
            @pl.when(reaches(offset))
            def _(offset=offset):
                halo_copy(v, offset).start()

    def halo_wait(v, part):
        for offset in part:
            @pl.when(reaches(offset))
            def _(offset=offset):
                halo_copy(v, offset).wait_send()
                halo_copy(v, minus(offset)).wait_recv()

    def total(value):
        return jnp.sum(value, axis=1, keepdims=True)

    def spread(value):
        return jnp.broadcast_to(value, zero.shape)

    def turned(tile, by):
        by = by % nz
        return pltpu.roll(tile, by, 1) if by else tile

    def emit(v, tile_of, centre=None):
        def step(x, edge):
            for y in range(ny):
                tile = tile_of(x, y)
                if centre is not None:
                    tile = tile - centre
                pads[v, x + 1, y + 1] = tile.astype(bf16)
                r = 2 * (x * ny + y)
                edge = jnp.where(lane == r, tile[:, nz - 1:nz], edge)
                edge = jnp.where(lane == r + 1, tile[:, 0:1], edge)
            return edge
        edge_out[v] = lax.fori_loop(0, nx, step, zero).astype(bf16)

    first_lanes = jnp.logical_or(lane == 0, lane == nz - 1)
    last_lanes = jnp.logical_or(lane == 2 * ny + 1, lane == 2 * ny + 2)

    def by_row(first, middle, last):
        return jnp.where(first_lanes, first, jnp.where(last_lanes, last, middle))

    def collect(v, part):
        for dx in (0,) if part is sides else (-1, 1):
            low, high = [[edge_in[v, code((-dx, -dy, -dz))] for dy in (-1, 0, 1)]
                         for dz in (-1, 1)]
            for x in range(1, nx + 1) if dx == 0 else (0,) if dx < 0 else (nx + 1,):
                base = (nx - 1, x - 1, 0)[dx + 1] * ny
                moves = (-2 * (base + ny), -2 * base, 2 * ny - 2 * base)
                got = [jnp.where(odd, turned(h, by), turned(l, by + 2))
                       for l, h, by in zip(low, high, moves)]
                cols[v, x] = by_row(*got)

    row_of_lane = jnp.where(lane == nz - 1, 0, lax.div(lane + 1, 2))
    low_y = jnp.where(me[1] > 0, 0, 1)
    high_y = jnp.where(me[1] < sizes[1] - 1, wide, wide - 1)
    low_z = jnp.where(me[2] > 0, 1, 0)
    high_z = jnp.where(me[2] < sizes[2] - 1, 1, 0)
    keep_edge = jnp.where(jnp.logical_and(row_of_lane >= low_y, row_of_lane < high_y),
                          jnp.where(odd, high_z, low_z), 0)

    def build(tile_of, shifted, turn, part):
        inner = part is sides

        def step(i, carry):
            if inner:
                x, x_ok = i + 1, None
            else:
                x = i * (nx + 1)
                x_ok = jnp.where(i == 0, me[0], sizes[0] - 1 - me[0]) > 0

            def both(flag):
                return flag if x_ok is None else jnp.logical_and(x_ok, flag)
            limits = {0: jnp.where(both(me[1] > 0), nz, 0),
                      wide - 1: jnp.where(both(me[1] < sizes[1] - 1), nz, 0)}
            middle = None if inner else jnp.where(x_ok, nz, 0)
            least = 1 if inner else jnp.where(x_ok, 1, 2)
            edge = tile_of(x, wide, inner)
            edge = jnp.where(keep_edge >= least, edge, jnp.zeros_like(edge)).astype(bf16)
            for y in range(wide):
                tile = tile_of(x, y, inner)
                limit = limits.get(y, middle)
                if limit is not None:
                    tile = jnp.where(lane < limit, tile, jnp.zeros_like(tile))
                tile = tile.astype(bf16)
                ends = turned(edge, -2 * y)
                low = jnp.where(lane == 0, ends, turned(tile, 1))
                high = jnp.where(lane == nz - 1, ends, turned(tile, -1))
                row = x * wide + y
                shifted[row, 0:chan] = high if turn else low
                shifted[row, chan:2 * chan] = tile
                shifted[row, 2 * chan:] = low if turn else high
            return carry
        lax.fori_loop(0, nx if inner else 2, step, 0)

    def raw_tiles(v):
        def tile_of(x, y, inner):
            return cols[v, x] if isinstance(y, int) and y == wide else pads[v, x, y]
        return tile_of

    def centred(v, k, full):
        def tile_of(x, y, inner):
            if not isinstance(y, int):
                return pads[v, x, y].astype(f32) + offs[k, x, 1]
            if y == wide:
                return cols[v, x].astype(f32) + offs[k, x, 3]
            if inner and 0 < y < wide - 1:
                return full[x - 1, y - 1] + offs[k, x, 1]
            kind = 0 if y == 0 else 2 if y == wide - 1 else 1
            return pads[v, x, y].astype(f32) + offs[k, x, kind]
        return tile_of

    def halo_rows(fn, part):
        if part is faces:
            def step(i, carry):
                for y in range(wide):
                    fn(i * (nx + 1), y, False)
                return carry
            lax.fori_loop(0, 2, step, 0)
        else:
            for x in range(1, nx + 1):
                for y in (0, wide - 1):
                    fn(x, y, True)

    def xs_of(part):
        return range(1, nx + 1) if part is sides else (0, nx + 1)

    def stack_rows(shifted, a, y, deep):
        parts = []
        for yi in range(deep + 2):
            parts.append(jnp.concatenate(
                [shifted[(x + a) * wide + y + yi] for x in range(nx)], axis=1))
        return parts

    def conv_rows(shifted, w, finish, init):
        def step(i, carry):
            y0 = i * DEEP
            data = jnp.concatenate(
                [p for a in range(3) for p in stack_rows(shifted, a, y0, DEEP)], axis=0)
            o = jnp.dot(mats[w], data, preferred_element_type=f32)
            for x in range(nx):
                for u in range(DEEP):
                    carry = finish(
                        x, y0 + u, o[u * chan:(u + 1) * chan, x * nz:(x + 1) * nz], carry)
            return carry
        return lax.fori_loop(0, ny // DEEP, step, init, unroll=2)

    def conv_stats(shifted, w, full):
        def finish(x, y, o, carry):
            full[x, y] = o
            return carry[0] + o, carry[1] + o * o
        return conv_rows(shifted, w, finish, (zero, zero))

    def row_of(values):
        tile = zero
        for k, value in enumerate(values):
            tile = jnp.where(lane == k * chan + chan_of, value, tile)
        return jnp.sum(tile, axis=0, keepdims=True)

    def column(row, k):
        return total(jnp.where(lane == k * chan + chan_of, row, 0.0))

    def all_start(buf, value, send, recv):
        buf[rank] = value
        for offset in others:
            pltpu.make_async_remote_copy(
                src_ref=buf.at[rank], dst_ref=buf.at[rank], send_sem=send,
                recv_sem=recv, device_id=ids(at_offset(offset)), device_id_type=MESH).start()

    def wait_bytes(buf, *sems):
        some = buf.at[pl.ds(0, count - 1)]
        for sem in sems:
            pltpu.make_async_copy(some, some, sem).wait()

    def tree(values):
        while len(values) > 1:
            values = [values[i] + values[i + 1] if i + 1 < len(values) else values[i]
                      for i in range(0, len(values), 2)]
        return values[0]

    def sums_start(j, values):
        all_start(slots.at[j], row_of([total(v) for v in values]), sum_send.at[j],
                  sum_recv.at[j])

    def sums_finish(j):
        wait_bytes(slots.at[j], sum_recv.at[j], sum_send.at[j])
        return tree([slots[j, r] for r in range(count)])

    def norm(row):
        mean = column(row, 0) / voxels
        var = column(row, 1) / voxels - mean * mean
        return spread(mean), spread(lax.rsqrt(var + EPSILON))

    def rounded(value):
        return spread(value / local).astype(bf16).astype(f32)

    def centre_of(sums):
        return rounded(total(sums[0]))

    def set_offsets(k, j, mean, part):
        def off(offset):
            return rounded(column(slots[j, rank_of(at_offset(offset))], 0)) - mean
        for dx in (0,) if part is sides else (-1, 1):
            rows = [-mean if dx == 0 and dy == 0 else off((dx, dy, 0)) for dy in (-1, 0, 1)]
            edges = by_row(*[jnp.where(odd, off((dx, dy, 1)), off((dx, dy, -1)))
                             for dy in (-1, 0, 1)])
            for x in range(1, nx + 1) if dx == 0 else (0,) if dx < 0 else (nx + 1,):
                for kind, value in enumerate(rows + [edges]):
                    offs[k, x, kind] = value

    def pieces(value):
        for u in range(tiles * (chan // 8)):
            r, t = u // tiles, u % tiles
            yield u // units, (u % units) * 8, r, t

    def spread_units(unit, slot, send, recv):
        for place, at, r, t in pieces(wsum):
            unit[place, pl.ds(at, 8)] = wsum[
                r * 8:r * 8 + 8, t * nz:(t + 1) * nz].astype(unit.dtype)
        slot[rank] = unit[rank]
        for offset in others:
            to = at_offset(offset)
            pltpu.make_async_remote_copy(
                src_ref=unit.at[rank_of(to)], dst_ref=slot.at[rank], send_sem=send,
                recv_sem=recv, device_id=ids(to), device_id_type=MESH).start()

    def gather_units(slot, send, recv):
        wait_bytes(slot, recv, send)
        return tree([slot[r].astype(f32) for r in range(count)])

    def share(j, value):
        all_start(wfull.at[j], value.astype(bf16), w_send.at[j], w_recv.at[j])

    def spell(j, out):
        wait_bytes(wfull.at[j], w_recv.at[j], w_send.at[j])
        for place, at, r, t in pieces(wsum):
            piece = wfull[j, place, pl.ds(at, 8)].astype(f32)
            for k in range(nz // chan):
                tap = t * (nz // chan) + k
                if tap < 27:
                    out[tap, pl.ds(r * 8, 8)] = piece[:, k * chan:(k + 1) * chan]

    def wgrad(delta_of, shifted, ones=False):
        cuts = []
        for g in range(ny // DEEP):
            for x in range(nx):
                parts = [delta_of(x, g * DEEP + u) for u in range(DEEP)]
                if ones:
                    parts.append(jnp.ones((16, nz), bf16))
                cuts.append(jnp.concatenate(parts, axis=0))
        delta = jnp.concatenate(cuts, axis=1)
        span = 3 * chan
        for a in range(3):
            groups = [jnp.concatenate(stack_rows(shifted, a, g * DEEP, DEEP), axis=0)
                      for g in range(ny // DEEP)]
            o = lax.dot_general(
                delta, jnp.concatenate(groups, axis=1), (((1,), (1,)), ((), ())),
                preferred_element_type=f32)
            for ty in range(3):
                at = (a * 3 + ty) * span
                wsum[:, at:at + span] = tree(
                    [o[u * chan:(u + 1) * chan, (u + ty) * span:(u + ty + 1) * span]
                     for u in range(DEEP)])
                if ones:
                    xsum[:, at:at + span] = tree(
                        [o[DEEP * chan:DEEP * chan + 1, (u + ty) * span:(u + ty + 1) * span]
                         for u in range(DEEP)])

    def take(k):
        def step(c, carry):
            at_row = pl.multiple_of(c * pitch, 8)
            for x in range(nx):
                tall[pl.ds(at_row + x * ny, ny)] = raw[k, c, x].astype(f32)
            return carry
        lax.fori_loop(0, chan, step, 0, unroll=4)

        def tile_of(x, y):
            return tall[pl.ds(x * ny + y, chan, stride=pitch)]
        return tile_of

    def give(out):
        def step(c, carry):
            at_row = pl.multiple_of(c * pitch, 8)
            for x in range(nx):
                out[c, x] = tall[pl.ds(at_row + x * ny, ny)].astype(bf16)
            return carry
        lax.fori_loop(0, chan, step, 0, unroll=4)

    def put_row(x, y, tile):
        tall[pl.ds(x * ny + y, chan, stride=pitch)] = tile

    def prepare(k):
        taps = [wraw[k, t].astype(f32) for t in range(27)]
        span = 3 * chan
        for turn in range(2):
            flat = jnp.concatenate(taps, axis=0).T if turn else jnp.concatenate(taps, axis=1)
            none = jnp.zeros((chan, span), f32)
            for u in range(DEEP):
                parts = []
                for a in range(3):
                    for yi in range(DEEP + 2):
                        tx, ty = (2 - a, 2 - yi + u) if turn else (a, yi - u)
                        at = (tx * 3 + ty) * span
                        parts.append(flat[:, at:at + span] if 0 <= ty < 3 else none)
                mats[2 * k + turn, u * chan:(u + 1) * chan] = jnp.concatenate(
                    parts, axis=1).astype(bf16)

    loads[0].wait()
    emit(XB, take(0))
    pl.semaphore_wait(barrier, count - 1)
    halo_start(XB)
    loads[2].wait()
    emit(XA, take(1))
    halo_start(XA)
    loads[3].wait()
    emit(GO, take(2))
    loads[1].wait()
    prepare(0)
    loads[4].wait()
    prepare(1)
    for k in range(5, 9):
        loads[k].wait()

    def gain(k):
        value = spread(jnp.concatenate([gains[k]] * (nz // chan), axis=1))
        return spread(column(value, 0))
    gain_one, bias_one, gain_two, bias_two = [gain(k) for k in range(4)]

    for part in (sides, faces):
        halo_wait(XB, part)
        collect(XB, part)
        build(raw_tiles(XB), shift_xb, False, part)
    sums = conv_stats(shift_xb, 0, c1b)
    sums_start(0, sums)
    emit(C1B, lambda x, y: c1b[x, y], centre_of(sums))
    halo_start(C1B)

    for part in (sides, faces):
        halo_wait(XA, part)
        collect(XA, part)
        build(raw_tiles(XA), shift_a, False, part)
    sums = conv_stats(shift_a, 0, c1a)
    sums_start(1, sums)
    emit(C1A, lambda x, y: c1a[x, y], centre_of(sums))
    halo_start(C1A)

    def silu(z):
        return z * jax.nn.sigmoid(z)

    mean_one, scale_one = norm(sums_finish(0))
    steep_one = gain_one * scale_one
    tile_1b = centred(C1B, 0, c1b)

    def z_one(x, y, inner):
        return tile_1b(x, y, inner) * steep_one + bias_one
    for part in (sides, faces):
        set_offsets(0, 0, mean_one, part)
        halo_wait(C1B, part)
        collect(C1B, part)
        build(lambda *at: silu(z_one(*at)), shift_hb, False, part)
    sums = conv_stats(shift_hb, 2, c2b)
    sums_start(2, sums)
    emit(C2B, lambda x, y: c2b[x, y], centre_of(sums))
    halo_start(C2B)
    halo_start(GO)

    mean_a, scale_a = norm(sums_finish(1))
    steep_a = gain_one * scale_a
    tile_1a = centred(C1A, 1, c1a)
    for part in (sides, faces):
        set_offsets(1, 1, mean_a, part)
        halo_wait(C1A, part)
        collect(C1A, part)
        build(lambda *at: silu(tile_1a(*at) * steep_a + bias_one), shift_a, False, part)
    sums = conv_stats(shift_a, 2, c2a)
    sums_start(3, sums)

    mean_two, scale_two = norm(sums_finish(2))
    steep_two = gain_two * scale_two

    def own_two(x, carry):
        sd, sx = carry
        for y in range(ny):
            c = c2b[x, y] - mean_two
            d = pads[GO, x + 1, y + 1].astype(f32) * slope_of(c * steep_two + bias_two)
            fd2[x + 1, y + 1] = d
            sd, sx = sd + d, sx + d * c
        return sd, sx
    sd, sx = lax.fori_loop(0, nx, own_two, (zero, zero))
    sums_start(4, (sx * scale_two, sd))

    wgrad(lambda x, y: ((c1b[x, y] - mean_one) * scale_one).astype(bf16), shift_xb, True)
    spread_units(unit_f.at[0], slot_f.at[0], w_send.at[2], w_recv.at[2])
    all_start(xfull, jnp.concatenate(
        [xsum[:, t * nz:(t + 1) * nz] for t in range(tiles)]
        + [jnp.zeros((8 - tiles % 8, nz), f32)], axis=0), w_send.at[3], w_recv.at[3])

    tile_2b = centred(C2B, 2, c2b)
    tile_go = raw_tiles(GO)

    def d_two(*at):
        return tile_go(*at).astype(f32) * slope_of(tile_2b(*at) * steep_two + bias_two)

    def halo_two(x, y, inner):
        fd2[x, y] = d_two(x, y, inner)

    for part in (sides, faces):
        set_offsets(2, 2, mean_two, part)
        halo_wait(C2B, part)
        halo_wait(GO, part)
        collect(C2B, part)
        collect(GO, part)
        halo_rows(halo_two, part)
        for x in xs_of(part):
            dcols[D2, x] = d_two(x, wide, part is sides)

    mean_a2, scale_a2 = norm(sums_finish(3))
    steep_a2 = gain_two * scale_a2

    def finish_a(x, carry):
        for y in range(ny):
            put_row(x, y, silu((c2a[x, y] - mean_a2) * steep_a2 + bias_two))
        return carry
    lax.fori_loop(0, nx, finish_a, 0)
    give(ya)

    row_two = sums_finish(4)
    sx2 = spread(column(row_two, 0) / voxels) * scale_two
    sd2 = spread(column(row_two, 1) / voxels)

    def dc_two(x, y, inner):
        d = dcols[D2, x] if y == wide else fd2[x, y]
        return steep_two * (d - sd2 - tile_2b(x, y, inner) * sx2)
    build(dc_two, shift_d, True, sides)
    build(dc_two, shift_d, True, faces)

    def back(x, y, o, carry):
        sd, sx = carry
        e1[x, y] = o
        c = c1b[x, y] - mean_one
        d = o * slope_of(c * steep_one + bias_one)
        fd1[x + 1, y + 1] = d
        d1h[x, y] = d.astype(bf16)
        return sd + d, sx + d * c
    sd, sx = conv_rows(shift_d, 3, back, (zero, zero))
    sums_start(5, (sx * scale_one, sd))
    wgrad(lambda x, y: d1h[x, y], shift_xb)
    spread_units(unit_f.at[1], slot_f.at[1], w_send.at[4], w_recv.at[4])
    emit(E1, lambda x, y: e1[x, y])
    halo_start(E1)
    wgrad(lambda x, y: shift_d[(x + 1) * wide + y + 1, chan:2 * chan], shift_hb)
    spread_units(unit_h, slot_h, w_send.at[5], w_recv.at[5])
    along = gather_units(slot_f.at[0], w_send.at[2], w_recv.at[2])
    wait_bytes(xfull, w_recv.at[3], w_send.at[3])
    plain = tree([xfull[r] for r in range(count)])
    xfull[rank] = plain

    row_one = sums_finish(5)
    sx1_wide = spread(column(row_one, 0) / voxels)
    sx1 = sx1_wide * scale_one
    sd1 = spread(column(row_one, 1) / voxels)
    for k, value in enumerate((steep_one * factor, sd1, sx1_wide)):
        kcol[k] = value

    def halo_one(x, y, inner):
        fd1[x, y] = pads[E1, x, y].astype(f32) * slope_of(z_one(x, y, inner))

    def dc_one(x, y, inner):
        d = dcols[D1, x] if y == wide else fd1[x, y]
        return steep_one * (d - sd1 - tile_1b(x, y, inner) * sx1)

    halo_wait(E1, sides)
    collect(E1, sides)
    halo_rows(halo_one, sides)
    for x in xs_of(sides):
        dcols[D1, x] = cols[E1, x].astype(f32) * slope_of(z_one(x, wide, True))
    build(dc_one, shift_d, True, sides)

    straight = gather_units(slot_f.at[1], w_send.at[4], w_recv.at[4])
    mixed = []
    for q in range(units):
        u = rank * units + q
        r = pl.multiple_of(jnp.minimum(lax.div(u, tiles), chan // 8 - 1) * 8, 8)
        k, d, x = [kcol[i, pl.ds(r, 8)] for i in range(3)]
        part = slice(q * 8, q * 8 + 8)
        mixed.append(k * (straight[part] - d * xfull[rank, pl.ds(lax.rem(u, tiles), 1)]
                          - x * along[part]))
    share(0, jnp.concatenate(mixed, axis=0))
    share(1, gather_units(slot_h, w_send.at[5], w_recv.at[5]) * factor)

    halo_wait(E1, faces)
    collect(E1, faces)
    halo_rows(halo_one, faces)
    for x in xs_of(faces):
        dcols[D1, x] = cols[E1, x].astype(f32) * slope_of(z_one(x, wide, False))
    build(dc_one, shift_d, True, faces)

    def last(x, y, o, carry):
        put_row(x, y, o)
        return carry
    conv_rows(shift_d, 1, last, 0)
    give(dxb)
    for k, row in enumerate((row_one, row_two)):
        for j in range(2):
            gnorm[2 * k + j:2 * k + j + 1, :] = row[:, j * chan:(j + 1) * chan] * factor
    spell(0, gw1)
    spell(1, gw2)


def deliver(*refs):
    sem = refs[-1]
    half = (len(refs) - 1) // 2
    copies = [pltpu.make_async_copy(src, dst, sem.at[k])
              for k, (src, dst) in enumerate(zip(refs[:half], refs[half:-1]))]
    for copy in copies:
        copy.start()
    for copy in copies:
        copy.wait()


def body(sizes, x_a, x_b, w_first, w_second, gain_first, bias_first, gain_second, bias_second,
         grad_out):
    chan, nx, ny, nz = x_a.shape
    count = math.prod(sizes)
    voxels = float(nx * ny * nz * count)
    taps = 27 * chan
    bf16, f32 = jnp.bfloat16, jnp.float32
    tiles = -(-taps // nz)
    units = -(-tiles * (chan // 8) // count)
    full = (nx + 2, ny + 2, chan, nz)
    span = (nx + 2) * (ny + 2)
    grid = (nx, ny, chan, nz)
    vmem = pl.BlockSpec(memory_space=pltpu.VMEM)
    hbm = pl.BlockSpec(memory_space=pl.ANY)
    dma = pltpu.SemaphoreType.DMA
    shapes = (
        jax.ShapeDtypeStruct(x_a.shape, bf16),
        jax.ShapeDtypeStruct(x_a.shape, bf16),
        jax.ShapeDtypeStruct((27, chan, chan), f32),
        jax.ShapeDtypeStruct((27, chan, chan), f32),
        jax.ShapeDtypeStruct((4, chan), f32),
    )
    results = pl.pallas_call(
        functools.partial(kernel, sizes, voxels, units),
        out_shape=shapes,
        in_specs=[hbm] * 9,
        out_specs=[vmem] * 5,
        scratch_shapes=[
            pltpu.VMEM((3, chan, nx, ny, nz), bf16),
            pltpu.VMEM((2, 27, chan, chan), bf16),
            pltpu.VMEM((4, 1, chan), f32),
            pltpu.VMEM((chan * (nx * ny + 8), nz), f32),
            pltpu.VMEM((4, DEEP * chan, 9 * (DEEP + 2) * chan), bf16),
            pltpu.VMEM((7,) + full, bf16),
            pltpu.VMEM((7, chan, nz), bf16),
            pltpu.VMEM((7, 27, chan, nz), bf16),
            pltpu.VMEM((7, nx + 2, chan, nz), bf16),
            pltpu.VMEM((2, nx + 2, chan, nz), f32),
            pltpu.VMEM((3, nx + 2, 4, chan, nz), f32),
        ] + [pltpu.VMEM((span, 3 * chan, nz), bf16)] * 4
        + [pltpu.VMEM(full, f32)] * 2
        + [pltpu.VMEM(grid, f32)] * 5
        + [
            pltpu.VMEM(grid, bf16),
            pltpu.VMEM((6, count, 1, nz), f32),
            pltpu.VMEM((1, tiles * nz), f32),
            pltpu.VMEM((count, -(-tiles // 8) * 8, nz), f32),
            pltpu.VMEM((3, chan, nz), f32),
            pltpu.VMEM((chan, tiles * nz), f32),
            pltpu.VMEM((count, 8 * units, nz), bf16),
            pltpu.VMEM((count, 8 * units, nz), bf16),
            pltpu.VMEM((2, count, 8 * units, nz), f32),
            pltpu.VMEM((2, count, 8 * units, nz), f32),
            pltpu.VMEM((2, count, 8 * units, nz), bf16),
            dma((9,)),
            dma((7, 27)), dma((7, 27)),
            dma((6,)), dma((6,)),
            dma((6,)), dma((6,)),
        ],
        compiler_params=pltpu.CompilerParams(
            collective_id=0, has_side_effects=True, vmem_limit_bytes=56 * 1024 * 1024),
    )(
        x_a, x_b, grad_out,
        w_first.reshape(27, chan, chan), w_second.reshape(27, chan, chan),
        gain_first.reshape(1, chan), bias_first.reshape(1, chan),
        gain_second.reshape(1, chan), bias_second.reshape(1, chan),
    )
    y_a, dx_b, gw1, gw2, gnorm = pl.pallas_call(
        deliver,
        out_shape=shapes,
        in_specs=[vmem] * 5,
        out_specs=[hbm] * 5,
        scratch_shapes=[dma((5,))],
    )(*results)
    cube = (3, 3, 3, chan, chan)
    return y_a, dx_b, gw1.reshape(cube), gw2.reshape(cube), gnorm


def solution(mesh):
    sizes = tuple(mesh.shape[a] for a in AXES)
    split = P(None, *AXES)
    return jax.shard_map(
        functools.partial(body, sizes),
        mesh=mesh,
        in_specs=(split, split, P(), P(), P(), P(), P(), P(), split),
        out_specs=(split, split, P(), P(), P()),
        check_vma=False,
    )
```

time: 74.2 us -> 64.2 us (0.87)
  Pallas kernels: 73.4 us -> 63.3 us
    pallas_call x1, Pallas kernels: 70.9 us -> 60.8 us  [body(): pl.pallas_call(functools.partial(kernel, sizes, voxels, units), out_shape...]
where the time goes in v2:
time: 64.2 us; the launch traced here: 64.1 us
  Pallas kernels  63.3 us (99%)
  between operations  0.8 us (1%)
    pallas_call x1, Pallas kernels, body(): pl.pallas_call(functools.partial(kernel, sizes, voxels, units), out_shape...  60.8 us
    pallas_call x1, Pallas kernels, body(): pl.pallas_call(deliver, out_shape=shapes, in_specs=[vmem] * 5, out_specs=...  2.44 us

profile of v2, /device:TPU:0, one launch (start us, length us, event | category | flops | bytes accessed | tf_op | source)
XLA Modules:
  0.0 64.1 jit_solution(1084947747311526208)
XLA Ops:
  0.6 60.8 %shard_map.128 = (bf16[32,2,16,128]{3,2,1,0:T(8,128)(2,1)}, bf16[32,2,16,128]{3,2,1,0:T(8,128)(2,1)}, f32[27,32,32]{2,1,0:T(8,128)}, f32[27,32,32]{2,1,0:T(8,128)}, f32[4,32]{1,0:T(4,128)}) custom-call(bf16[32,2,16,128]{3,2,1,0:T(8,128)(2,1)} %xa.1, bf16[32,2,16,128]{3,2,1,0:T(8,128)(2,1)} %xb.1, bf16[32,2,16,128]{3,2,1,0:T(8,128)(2,1)} %go.1, ...), custom_call_target="tpu_custom_call" | custom-call | tf_op jit(solution)/shard_map/pallas_call | solution.py:660
  61.5 2.4 %shard_map.129 = (bf16[32,2,16,128]{3,2,1,0:T(8,128)(2,1)}, bf16[32,2,16,128]{3,2,1,0:T(8,128)(2,1)}, f32[27,32,32]{2,1,0:T(8,128)}, f32[27,32,32]{2,1,0:T(8,128)}, f32[4,32]{1,0:T(4,128)}) custom-call(bf16[32,2,16,128]{3,2,1,0:T(8,128)(2,1)} %get-tuple-element.15.refs_0_, bf16[32,2,16,128]{3,2,1,0:T(8,128)(2,1)} %get-tuple-element.16.refs_1_, ...), custom_call_target="tpu_custom_call" | custom-call | tf_op jit(solution)/shard_map/pallas_call | solution.py:705

commit v3 on v2

--- a/solution.py
+++ b/solution.py
@@ -38,8 +38,8 @@
     ya, dxb, gw1, gw2, gnorm,
     raw, wraw, gains, tall, mats, pads, edge_out, edge_in, cols, dcols, offs,
     shift_xb, shift_a, shift_hb, shift_d,
-    fd2, fd1, c1b, c1a, c2b, c2a, e1, d1h, slots, xsum, xfull, kcol, wsum,
-    unit_h, slot_h, unit_f, slot_f, wfull,
+    fd2, fd1, c1b, c1a, c2b, c2a, e1, d1h, slots, xsum, plain, kcol, wsum,
+    unit_x, slot_x, line_x, unit_f, slot_f, line_f, unit_h, slot_h, line_h, wfull,
     load_sem, halo_send, halo_recv, sum_send, sum_recv, w_send, w_recv,
 ):
     chan, nx, ny, nz = raw.shape[1:]
@@ -284,8 +284,8 @@
                 src_ref=buf.at[rank], dst_ref=buf.at[rank], send_sem=send,
                 recv_sem=recv, device_id=ids(at_offset(offset)), device_id_type=MESH).start()
 
-    def wait_bytes(buf, *sems):
-        some = buf.at[pl.ds(0, count - 1)]
+    def wait_bytes(buf, n, *sems):
+        some = buf.at[pl.ds(0, n - 1)]
         for sem in sems:
             pltpu.make_async_copy(some, some, sem).wait()
 
@@ -300,7 +300,7 @@
                   sum_recv.at[j])
 
     def sums_finish(j):
-        wait_bytes(slots.at[j], sum_recv.at[j], sum_send.at[j])
+        wait_bytes(slots.at[j], count, sum_recv.at[j], sum_send.at[j])
         return tree([slots[j, r] for r in range(count)])
 
     def norm(row):
@@ -325,32 +325,55 @@
                 for kind, value in enumerate(rows + [edges]):
                     offs[k, x, kind] = value
 
-    def pieces(value):
+    plane = sizes[1] * sizes[2]
+    in_plane = lax.rem(rank, plane)
+    plane_others = [o for o in others if o[0] == 0]
+    line_others = [o for o in others if o[1] == 0 and o[2] == 0]
+
+    def pieces():
         for u in range(tiles * (chan // 8)):
             r, t = u // tiles, u % tiles
             yield u // units, (u % units) * 8, r, t
 
-    def spread_units(unit, slot, send, recv):
-        for place, at, r, t in pieces(wsum):
+    def send_some(group, src_of, buf, at, send, recv):
+        for offset in group:
+            to = at_offset(offset)
+            pltpu.make_async_remote_copy(
+                src_ref=src_of(to), dst_ref=buf.at[at], send_sem=send,
+                recv_sem=recv, device_id=ids(to), device_id_type=MESH).start()
+
+    def plane_start(j, unit, slot, with_x=False):
+        for place, at, r, t in pieces():
             unit[place, pl.ds(at, 8)] = wsum[
                 r * 8:r * 8 + 8, t * nz:(t + 1) * nz].astype(unit.dtype)
-        slot[rank] = unit[rank]
-        for offset in others:
-            to = at_offset(offset)
-            pltpu.make_async_remote_copy(
-                src_ref=unit.at[rank_of(to)], dst_ref=slot.at[rank], send_sem=send,
-                recv_sem=recv, device_id=ids(to), device_id_type=MESH).start()
-
-    def gather_units(slot, send, recv):
-        wait_bytes(slot, recv, send)
-        return tree([slot[r].astype(f32) for r in range(count)])
+        if with_x:
+            for place in range(plane):
+                for t in range(tiles):
+                    unit[place, pl.ds(8 * units + t, 1)] = xsum[:, t * nz:(t + 1) * nz]
+        slot[in_plane] = unit[in_plane]
+        send_some(plane_others, lambda to: unit.at[to[1] * sizes[2] + to[2]], slot, in_plane,
+                  w_send.at[j], w_recv.at[j])
+
+    def added(j, buf, n):
+        wait_bytes(buf, n, w_recv.at[j], w_send.at[j])
+        return tree([buf[r].astype(f32) for r in range(n)])
+
+    def line_start(j, slot, line):
+        line[me[0]] = added(j, slot, plane).astype(line.dtype)
+        send_some(line_others, lambda to: line.at[me[0]], line, me[0],
+                  w_send.at[j + 1], w_recv.at[j + 1])
+
+    def line_finish(j, line):
+        return added(j + 1, line, sizes[0])
 
     def share(j, value):
-        all_start(wfull.at[j], value.astype(bf16), w_send.at[j], w_recv.at[j])
+        wfull[j, in_plane] = value.astype(bf16)
+        send_some(plane_others, lambda to: wfull.at[j, in_plane], wfull.at[j], in_plane,
+                  w_send.at[j], w_recv.at[j])
 
     def spell(j, out):
-        wait_bytes(wfull.at[j], w_recv.at[j], w_send.at[j])
-        for place, at, r, t in pieces(wsum):
+        wait_bytes(wfull.at[j], plane, w_recv.at[j], w_send.at[j])
+        for place, at, r, t in pieces():
             piece = wfull[j, place, pl.ds(at, 8)].astype(f32)
             for k in range(nz // chan):
                 tap = t * (nz // chan) + k
@@ -479,7 +502,6 @@
     sums_start(2, sums)
     emit(C2B, lambda x, y: c2b[x, y], centre_of(sums))
     halo_start(C2B)
-    halo_start(GO)
 
     mean_a, scale_a = norm(sums_finish(1))
     steep_a = gain_one * scale_a
@@ -505,12 +527,10 @@
         return sd, sx
     sd, sx = lax.fori_loop(0, nx, own_two, (zero, zero))
     sums_start(4, (sx * scale_two, sd))
+    halo_start(GO)
 
     wgrad(lambda x, y: ((c1b[x, y] - mean_one) * scale_one).astype(bf16), shift_xb, True)
-    spread_units(unit_f.at[0], slot_f.at[0], w_send.at[2], w_recv.at[2])
-    all_start(xfull, jnp.concatenate(
-        [xsum[:, t * nz:(t + 1) * nz] for t in range(tiles)]
-        + [jnp.zeros((8 - tiles % 8, nz), f32)], axis=0), w_send.at[3], w_recv.at[3])
+    plane_start(2, unit_x, slot_x, True)
 
     tile_2b = centred(C2B, 2, c2b)
     tile_go = raw_tiles(GO)
@@ -561,16 +581,13 @@
         return sd + d, sx + d * c
     sd, sx = conv_rows(shift_d, 3, back, (zero, zero))
     sums_start(5, (sx * scale_one, sd))
-    wgrad(lambda x, y: d1h[x, y], shift_xb)
-    spread_units(unit_f.at[1], slot_f.at[1], w_send.at[4], w_recv.at[4])
     emit(E1, lambda x, y: e1[x, y])
     halo_start(E1)
+    wgrad(lambda x, y: d1h[x, y], shift_xb)
+    plane_start(4, unit_f, slot_f)
+    line_start(2, slot_x, line_x)
     wgrad(lambda x, y: shift_d[(x + 1) * wide + y + 1, chan:2 * chan], shift_hb)
-    spread_units(unit_h, slot_h, w_send.at[5], w_recv.at[5])
-    along = gather_units(slot_f.at[0], w_send.at[2], w_recv.at[2])
-    wait_bytes(xfull, w_recv.at[3], w_send.at[3])
-    plain = tree([xfull[r] for r in range(count)])
-    xfull[rank] = plain
+    plane_start(6, unit_h, slot_h)
 
     row_one = sums_finish(5)
     sx1_wide = spread(column(row_one, 0) / voxels)
@@ -593,17 +610,7 @@
         dcols[D1, x] = cols[E1, x].astype(f32) * slope_of(z_one(x, wide, True))
     build(dc_one, shift_d, True, sides)
 
-    straight = gather_units(slot_f.at[1], w_send.at[4], w_recv.at[4])
-    mixed = []
-    for q in range(units):
-        u = rank * units + q
-        r = pl.multiple_of(jnp.minimum(lax.div(u, tiles), chan // 8 - 1) * 8, 8)
-        k, d, x = [kcol[i, pl.ds(r, 8)] for i in range(3)]
-        part = slice(q * 8, q * 8 + 8)
-        mixed.append(k * (straight[part] - d * xfull[rank, pl.ds(lax.rem(u, tiles), 1)]
-                          - x * along[part]))
-    share(0, jnp.concatenate(mixed, axis=0))
-    share(1, gather_units(slot_h, w_send.at[5], w_recv.at[5]) * factor)
+    line_start(4, slot_f, line_f)
 
     halo_wait(E1, faces)
     collect(E1, faces)
@@ -611,12 +618,26 @@
     for x in xs_of(faces):
         dcols[D1, x] = cols[E1, x].astype(f32) * slope_of(z_one(x, wide, False))
     build(dc_one, shift_d, True, faces)
+    line_start(6, slot_h, line_h)
 
     def last(x, y, o, carry):
         put_row(x, y, o)
         return carry
     conv_rows(shift_d, 1, last, 0)
     give(dxb)
+    along = line_finish(2, line_x)
+    plain[...] = along[8 * units:]
+    straight = line_finish(4, line_f)
+    mixed = []
+    for q in range(units):
+        u = in_plane * units + q
+        r = pl.multiple_of(jnp.minimum(lax.div(u, tiles), chan // 8 - 1) * 8, 8)
+        k, d, x = [kcol[i, pl.ds(r, 8)] for i in range(3)]
+        part = slice(q * 8, q * 8 + 8)
+        mixed.append(k * (straight[part] - d * plain[pl.ds(lax.rem(u, tiles), 1)]
+                          - x * along[part]))
+    share(0, jnp.concatenate(mixed, axis=0))
+    share(1, line_finish(6, line_h) * factor)
     for k, row in enumerate((row_one, row_two)):
         for j in range(2):
             gnorm[2 * k + j:2 * k + j + 1, :] = row[:, j * chan:(j + 1) * chan] * factor
@@ -643,7 +664,8 @@
     taps = 27 * chan
     bf16, f32 = jnp.bfloat16, jnp.float32
     tiles = -(-taps // nz)
-    units = -(-tiles * (chan // 8) // count)
+    plane = sizes[1] * sizes[2]
+    units = -(-tiles * (chan // 8) // plane)
     full = (nx + 2, ny + 2, chan, nz)
     span = (nx + 2) * (ny + 2)
     grid = (nx, ny, chan, nz)
@@ -681,18 +703,23 @@
             pltpu.VMEM(grid, bf16),
             pltpu.VMEM((6, count, 1, nz), f32),
             pltpu.VMEM((1, tiles * nz), f32),
-            pltpu.VMEM((count, -(-tiles // 8) * 8, nz), f32),
+            pltpu.VMEM((8, nz), f32),
             pltpu.VMEM((3, chan, nz), f32),
             pltpu.VMEM((chan, tiles * nz), f32),
-            pltpu.VMEM((count, 8 * units, nz), bf16),
-            pltpu.VMEM((count, 8 * units, nz), bf16),
-            pltpu.VMEM((2, count, 8 * units, nz), f32),
-            pltpu.VMEM((2, count, 8 * units, nz), f32),
-            pltpu.VMEM((2, count, 8 * units, nz), bf16),
+            pltpu.VMEM((plane, 8 * units + 8, nz), f32),
+            pltpu.VMEM((plane, 8 * units + 8, nz), f32),
+            pltpu.VMEM((sizes[0], 8 * units + 8, nz), f32),
+            pltpu.VMEM((plane, 8 * units, nz), f32),
+            pltpu.VMEM((plane, 8 * units, nz), f32),
+            pltpu.VMEM((sizes[0], 8 * units, nz), f32),
+            pltpu.VMEM((plane, 8 * units, nz), bf16),
+            pltpu.VMEM((plane, 8 * units, nz), bf16),
+            pltpu.VMEM((sizes[0], 8 * units, nz), bf16),
+            pltpu.VMEM((2, plane, 8 * units, nz), bf16),
             dma((9,)),
             dma((7, 27)), dma((7, 27)),
             dma((6,)), dma((6,)),
-            dma((6,)), dma((6,)),
+            dma((8,)), dma((8,)),
         ],
         compiler_params=pltpu.CompilerParams(
             collective_id=0, has_side_effects=True, vmem_limit_bytes=56 * 1024 * 1024),

time: 64.2 us -> 57.1 us (0.89)
  Pallas kernels: 63.3 us -> 56.1 us
    pallas_call x1, Pallas kernels: 60.8 us -> 53.7 us  [body(): pl.pallas_call(functools.partial(kernel, sizes, voxels, units), out_shape...]
where the time goes in v3:
time: 57.1 us; the launch traced here: 56.9 us
  Pallas kernels  56.1 us (98%)
  between operations  0.8 us (1%)
    pallas_call x1, Pallas kernels, body(): pl.pallas_call(functools.partial(kernel, sizes, voxels, units), out_shape...  53.7 us
    pallas_call x1, Pallas kernels, body(): pl.pallas_call(deliver, out_shape=shapes, in_specs=[vmem] * 5, out_specs=...  2.44 us

profile of v3, /device:TPU:0, one launch (start us, length us, event | category | flops | bytes accessed | tf_op | source)
XLA Modules:
  0.0 56.9 jit_solution(14096955430867697038)
XLA Ops:
  0.6 53.7 %shard_map.128 = (bf16[32,2,16,128]{3,2,1,0:T(8,128)(2,1)}, bf16[32,2,16,128]{3,2,1,0:T(8,128)(2,1)}, f32[27,32,32]{2,1,0:T(8,128)}, f32[27,32,32]{2,1,0:T(8,128)}, f32[4,32]{1,0:T(4,128)}) custom-call(bf16[32,2,16,128]{3,2,1,0:T(8,128)(2,1)} %xa.1, bf16[32,2,16,128]{3,2,1,0:T(8,128)(2,1)} %xb.1, bf16[32,2,16,128]{3,2,1,0:T(8,128)(2,1)} %go.1, ...), custom_call_target="tpu_custom_call" | custom-call | tf_op jit(solution)/shard_map/pallas_call | solution.py:682
  54.3 2.4 %shard_map.129 = (bf16[32,2,16,128]{3,2,1,0:T(8,128)(2,1)}, bf16[32,2,16,128]{3,2,1,0:T(8,128)(2,1)}, f32[27,32,32]{2,1,0:T(8,128)}, f32[27,32,32]{2,1,0:T(8,128)}, f32[4,32]{1,0:T(4,128)}) custom-call(bf16[32,2,16,128]{3,2,1,0:T(8,128)(2,1)} %get-tuple-element.15.refs_0_, bf16[32,2,16,128]{3,2,1,0:T(8,128)(2,1)} %get-tuple-element.16.refs_1_, ...), custom_call_target="tpu_custom_call" | custom-call | tf_op jit(solution)/shard_map/pallas_call | solution.py:732

commit v4 on v3

--- a/solution.py
+++ b/solution.py
@@ -18,8 +18,12 @@
 DEEP = 4
 
 
+def sigmoid(z):
+    return 0.5 * jnp.tanh(0.5 * z) + 0.5
+
+
 def slope_of(z):
-    s = jax.nn.sigmoid(z)
+    s = sigmoid(z)
     return s * (1.0 + z * (1.0 - s))
 
 
@@ -40,7 +44,7 @@
     shift_xb, shift_a, shift_hb, shift_d,
     fd2, fd1, c1b, c1a, c2b, c2a, e1, d1h, slots, xsum, plain, kcol, wsum,
     unit_x, slot_x, line_x, unit_f, slot_f, line_f, unit_h, slot_h, line_h, wfull,
-    load_sem, halo_send, halo_recv, sum_send, sum_recv, w_send, w_recv,
+    bytes_of, load_sem, halo_send, halo_recv, sum_send, sum_recv, w_send, w_recv,
 ):
     chan, nx, ny, nz = raw.shape[1:]
     wide = ny + 2
@@ -62,7 +66,7 @@
     bf16, f32 = jnp.bfloat16, jnp.float32
 
     others = [(a, b, c) for a in range(sizes[0]) for b in range(sizes[1])
-              for c in range(sizes[2])][1:]
+              for c in range(sizes[2])][:0:-1]
 
     def at_offset(offset):
         return [lax.rem(m + o + s, s) for m, o, s in zip(me, offset, sizes)]
@@ -106,7 +110,7 @@
                 return (n, 0) if o > 0 else (1, n + 1)
             (sx, dx), (sy, dy) = cut(offset[0], nx), cut(offset[1], ny)
             src, dst = pads.at[v, sx, sy], pads.at[v, dx, dy]
-        m = code(offset)
+        m = 0 if offset[0] == 0 else 1
         return pltpu.make_async_remote_copy(
             src_ref=src, dst_ref=dst, send_sem=halo_send.at[v, m],
             recv_sem=halo_recv.at[v, m], device_id=to, device_id_type=MESH)
@@ -121,12 +125,27 @@
             def _(offset=offset):
                 halo_copy(v, offset).start()
 
+    near = [jnp.where(inside[k][-1], 1, 0) + jnp.where(inside[k][1], 1, 0) for k in range(3)]
+    cases = [(0,) if n == 1 else (1,) if n == 2 else (1, 2) for n in sizes]
+
     def halo_wait(v, part):
-        for offset in part:
-            @pl.when(reaches(offset))
-            def _(offset=offset):
-                halo_copy(v, offset).wait_send()
-                halo_copy(v, minus(offset)).wait_recv()
+        m = 0 if part is sides else 1
+        for a in ((0,) if part is sides else cases[0]):
+            for b in cases[1]:
+                for c in cases[2]:
+                    rows = b * nx + c * (1 + b) if part is sides else a * (
+                        ny + b + c * (1 + b))
+                    if not rows:
+                        continue
+                    flag = jnp.logical_and(near[1] == b, near[2] == c)
+                    if part is faces:
+                        flag = jnp.logical_and(flag, near[0] == a)
+
+                    @pl.when(flag)
+                    def _(rows=rows):
+                        some = bytes_of.at[pl.ds(0, rows)]
+                        for sem in (halo_recv.at[v, m], halo_send.at[v, m]):
+                            pltpu.make_async_copy(some, some, sem).wait()
 
     def total(value):
         return jnp.sum(value, axis=1, keepdims=True)
@@ -144,12 +163,13 @@
                 tile = tile_of(x, y)
                 if centre is not None:
                     tile = tile - centre
-                pads[v, x + 1, y + 1] = tile.astype(bf16)
+                tile = tile.astype(bf16)
+                pads[v, x + 1, y + 1] = tile
                 r = 2 * (x * ny + y)
                 edge = jnp.where(lane == r, tile[:, nz - 1:nz], edge)
                 edge = jnp.where(lane == r + 1, tile[:, 0:1], edge)
             return edge
-        edge_out[v] = lax.fori_loop(0, nx, step, zero).astype(bf16)
+        edge_out[v] = lax.fori_loop(0, nx, step, zero.astype(bf16))
 
     first_lanes = jnp.logical_or(lane == 0, lane == nz - 1)
     last_lanes = jnp.logical_or(lane == 2 * ny + 1, lane == 2 * ny + 2)
@@ -227,20 +247,10 @@
             return pads[v, x, y].astype(f32) + offs[k, x, kind]
         return tile_of
 
-    def halo_rows(fn, part):
-        if part is faces:
-            def step(i, carry):
-                for y in range(wide):
-                    fn(i * (nx + 1), y, False)
-                return carry
-            lax.fori_loop(0, 2, step, 0)
-        else:
-            for x in range(1, nx + 1):
-                for y in (0, wide - 1):
-                    fn(x, y, True)
-
-    def xs_of(part):
-        return range(1, nx + 1) if part is sides else (0, nx + 1)
+    def halo_rows(fn):
+        for x in range(1, nx + 1):
+            for y in (0, wide - 1):
+                fn(x, y, True)
 
     def stack_rows(shifted, a, y, deep):
         parts = []
@@ -485,7 +495,7 @@
     halo_start(C1A)
 
     def silu(z):
-        return z * jax.nn.sigmoid(z)
+        return z * sigmoid(z)
 
     mean_one, scale_one = norm(sums_finish(0))
     steep_one = gain_one * scale_one
@@ -541,15 +551,17 @@
     def halo_two(x, y, inner):
         fd2[x, y] = d_two(x, y, inner)
 
-    for part in (sides, faces):
-        set_offsets(2, 2, mean_two, part)
-        halo_wait(C2B, part)
-        halo_wait(GO, part)
-        collect(C2B, part)
-        collect(GO, part)
-        halo_rows(halo_two, part)
-        for x in xs_of(part):
-            dcols[D2, x] = d_two(x, wide, part is sides)
+    set_offsets(2, 2, mean_two, sides)
+    halo_wait(C2B, sides)
+    collect(C2B, sides)
+    halo_wait(GO, sides)
+    collect(GO, sides)
+    halo_rows(halo_two)
+    for x in range(1, nx + 1):
+        dcols[D2, x] = d_two(x, wide, True)
+    set_offsets(2, 2, mean_two, faces)
+    halo_wait(C2B, faces)
+    collect(C2B, faces)
 
     mean_a2, scale_a2 = norm(sums_finish(3))
     steep_a2 = gain_two * scale_a2
@@ -566,9 +578,15 @@
     sd2 = spread(column(row_two, 1) / voxels)
 
     def dc_two(x, y, inner):
-        d = dcols[D2, x] if y == wide else fd2[x, y]
-        return steep_two * (d - sd2 - tile_2b(x, y, inner) * sx2)
+        c = tile_2b(x, y, inner)
+        if not inner:
+            d = tile_go(x, y, inner).astype(f32) * slope_of(c * steep_two + bias_two)
+        else:
+            d = dcols[D2, x] if y == wide else fd2[x, y]
+        return steep_two * (d - sd2 - c * sx2)
     build(dc_two, shift_d, True, sides)
+    halo_wait(GO, faces)
+    collect(GO, faces)
     build(dc_two, shift_d, True, faces)
 
     def back(x, y, o, carry):
@@ -600,13 +618,18 @@
         fd1[x, y] = pads[E1, x, y].astype(f32) * slope_of(z_one(x, y, inner))
 
     def dc_one(x, y, inner):
-        d = dcols[D1, x] if y == wide else fd1[x, y]
-        return steep_one * (d - sd1 - tile_1b(x, y, inner) * sx1)
+        c = tile_1b(x, y, inner)
+        if inner:
+            d = dcols[D1, x] if y == wide else fd1[x, y]
+        else:
+            e = cols[E1, x] if y == wide else pads[E1, x, y]
+            d = e.astype(f32) * slope_of(c * steep_one + bias_one)
+        return steep_one * (d - sd1 - c * sx1)
 
     halo_wait(E1, sides)
     collect(E1, sides)
-    halo_rows(halo_one, sides)
-    for x in xs_of(sides):
+    halo_rows(halo_one)
+    for x in range(1, nx + 1):
         dcols[D1, x] = cols[E1, x].astype(f32) * slope_of(z_one(x, wide, True))
     build(dc_one, shift_d, True, sides)
 
@@ -614,9 +637,6 @@
 
     halo_wait(E1, faces)
     collect(E1, faces)
-    halo_rows(halo_one, faces)
-    for x in xs_of(faces):
-        dcols[D1, x] = cols[E1, x].astype(f32) * slope_of(z_one(x, wide, False))
     build(dc_one, shift_d, True, faces)
     line_start(6, slot_h, line_h)
 
@@ -670,7 +690,7 @@
     span = (nx + 2) * (ny + 2)
     grid = (nx, ny, chan, nz)
     vmem = pl.BlockSpec(memory_space=pltpu.VMEM)
-    hbm = pl.BlockSpec(memory_space=pl.ANY)
+    hbm = pl.BlockSpec(memory_space=pltpu.HBM)
     dma = pltpu.SemaphoreType.DMA
     shapes = (
         jax.ShapeDtypeStruct(x_a.shape, bf16),
@@ -716,25 +736,27 @@
             pltpu.VMEM((plane, 8 * units, nz), bf16),
             pltpu.VMEM((sizes[0], 8 * units, nz), bf16),
             pltpu.VMEM((2, plane, 8 * units, nz), bf16),
+            pltpu.VMEM((2 * (ny + 8), chan, nz), bf16),
             dma((9,)),
-            dma((7, 27)), dma((7, 27)),
+            dma((7, 2)), dma((7, 2)),
             dma((6,)), dma((6,)),
             dma((8,)), dma((8,)),
         ],
         compiler_params=pltpu.CompilerParams(
-            collective_id=0, has_side_effects=True, vmem_limit_bytes=56 * 1024 * 1024),
-    )(
+            collective_id=0, has_side_effects=True, vmem_limit_bytes=40 * 1024 * 1024),
+    )(*[pltpu.with_memory_space_constraint(v, pltpu.HBM) for v in (
         x_a, x_b, grad_out,
         w_first.reshape(27, chan, chan), w_second.reshape(27, chan, chan),
         gain_first.reshape(1, chan), bias_first.reshape(1, chan),
         gain_second.reshape(1, chan), bias_second.reshape(1, chan),
-    )
+    )])
     y_a, dx_b, gw1, gw2, gnorm = pl.pallas_call(
         deliver,
         out_shape=shapes,
         in_specs=[vmem] * 5,
         out_specs=[hbm] * 5,
         scratch_shapes=[dma((5,))],
+        compiler_params=pltpu.CompilerParams(vmem_limit_bytes=8 * 1024 * 1024),
     )(*results)
     cube = (3, 3, 3, chan, chan)
     return y_a, dx_b, gw1.reshape(cube), gw2.reshape(cube), gnorm

time: 57.1 us -> 51.4 us (0.900)
  Pallas kernels: 56.1 us -> 50.4 us
    pallas_call x1, Pallas kernels: 53.7 us -> 49.3 us  [body(): pl.pallas_call(functools.partial(kernel, sizes, voxels, units), out_shape...]
    pallas_call x1, Pallas kernels: 2.44 us -> 1.13 us  [body(): pl.pallas_call(deliver, out_shape=shapes, in_specs=[vmem] * 5, out_specs=...]
where the time goes in v4:
time: 51.4 us; the launch traced here: 51.2 us
  Pallas kernels  50.4 us (98%)
  between operations  0.8 us (2%)
    pallas_call x1, Pallas kernels, body(): pl.pallas_call(functools.partial(kernel, sizes, voxels, units), out_shape...  49.3 us
    pallas_call x1, Pallas kernels, body(): pl.pallas_call(deliver, out_shape=shapes, in_specs=[vmem] * 5, out_specs=...  1.13 us

profile of v4, /device:TPU:0, one launch (start us, length us, event | category | flops | bytes accessed | tf_op | source)
XLA Modules:
  0.0 51.2 jit_solution(12836746617842511026)
XLA Ops:
  0.6 49.3 %shard_map.128 = (bf16[32,2,16,128]{3,2,1,0:T(8,128)(2,1)S(1)}, bf16[32,2,16,128]{3,2,1,0:T(8,128)(2,1)S(1)}, f32[27,32,32]{2,1,0:T(8,128)S(1)}, f32[27,32,32]{2,1,0:T(8,128)S(1)}, f32[4,32]{1,0:T(4,128)S(1)}) custom-call(bf16[32,2,16,128]{3,2,1,0:T(8,128)(2,1)} %xa.1, bf16[32,2,16,128]{3,2,1,0:T(8,128)(2,1)} %xb.1, bf16[32,2,16,128]{3,2,1,0:T(8,128)(2,1)} %go.1, ...), custom_call_target="tpu_custom_call" | custom-call | tf_op jit(solution)/shard_map/pallas_call | solution.py:702
  49.9 1.1 %shard_map.129 = (bf16[32,2,16,128]{3,2,1,0:T(8,128)(2,1)}, bf16[32,2,16,128]{3,2,1,0:T(8,128)(2,1)}, f32[27,32,32]{2,1,0:T(8,128)}, f32[27,32,32]{2,1,0:T(8,128)}, f32[4,32]{1,0:T(4,128)}) custom-call(bf16[32,2,16,128]{3,2,1,0:T(8,128)(2,1)S(1)} %get-tuple-element.15.refs_0_, bf16[32,2,16,128]{3,2,1,0:T(8,128)(2,1)S(1)} %get-tuple-element.16.refs_1_, ...), custom_call_target="tpu_custom_call" | custom-call | tf_op jit(solution)/shard_map/pallas_call | solution.py:753

commit v5 on v4

--- a/solution.py
+++ b/solution.py
@@ -37,12 +37,12 @@
 
 
 def kernel(
-    sizes, voxels, units,
+    sizes, voxels,
     xa, xb, go, w1, w2, g1, b1, g2, b2,
     ya, dxb, gw1, gw2, gnorm,
     raw, wraw, gains, tall, mats, pads, edge_out, edge_in, cols, dcols, offs,
     shift_xb, shift_a, shift_hb, shift_d,
-    fd2, fd1, c1b, c1a, c2b, c2a, e1, d1h, slots, xsum, plain, kcol, wsum,
+    fd2, fd1, c1b, c1a, c2b, c2a, e1, d1h, slots, xsum, wsum,
     unit_x, slot_x, line_x, unit_f, slot_f, line_f, unit_h, slot_h, line_h, wfull,
     bytes_of, load_sem, halo_send, halo_recv, sum_send, sum_recv, w_send, w_recv,
 ):
@@ -99,52 +99,64 @@
             flag = jnp.logical_and(flag, more)
         return flag
 
-    def halo_copy(v, offset):
-        to = ids([me[k] + o for k, o in enumerate(offset)])
+    SIDES, FIRST, LAST = range(3)
+    split = ny // 2 + 1
+
+    def halo_pieces(v, offset):
         if offset[2]:
-            src, dst = edge_out.at[v], edge_in.at[v, code(offset)]
-        else:
-            def cut(o, n):
-                if o == 0:
-                    return pl.ds(1, n), pl.ds(1, n)
-                return (n, 0) if o > 0 else (1, n + 1)
-            (sx, dx), (sy, dy) = cut(offset[0], nx), cut(offset[1], ny)
-            src, dst = pads.at[v, sx, sy], pads.at[v, dx, dy]
-        m = 0 if offset[0] == 0 else 1
-        return pltpu.make_async_remote_copy(
-            src_ref=src, dst_ref=dst, send_sem=halo_send.at[v, m],
-            recv_sem=halo_recv.at[v, m], device_id=to, device_id_type=MESH)
+            part = FIRST if offset[0] else SIDES
+            return [(part, edge_out.at[v], edge_in.at[v, code(offset)])]
+
+        def cut(o, n):
+            if o == 0:
+                return pl.ds(1, n), pl.ds(1, n)
+            return (n, 0) if o > 0 else (1, n + 1)
+        (sx, dx), (sy, dy) = cut(offset[0], nx), cut(offset[1], ny)
+        if offset[0] and not offset[1]:
+            return [(part, pads.at[v, sx, rows], pads.at[v, dx, rows])
+                    for part, rows in ((FIRST, pl.ds(1, split)),
+                                       (LAST, pl.ds(1 + split, ny - split)))]
+        part = FIRST if offset[0] else SIDES
+        return [(part, pads.at[v, sx, sy], pads.at[v, dx, dy])]
 
     order = sorted(OFFSETS, key=lambda o: (o[1] == 0 and o[2] == 0, o[0] != 0))
-    sides = [o for o in order if o[0] == 0]
-    faces = [o for o in order if o[0] != 0]
 
     def halo_start(v):
         for offset in order:
+            to = ids([me[k] + o for k, o in enumerate(offset)])
+
             @pl.when(reaches(offset))
-            def _(offset=offset):
-                halo_copy(v, offset).start()
+            def _(offset=offset, to=to):
+                for part, src, dst in halo_pieces(v, offset):
+                    pltpu.make_async_remote_copy(
+                        src_ref=src, dst_ref=dst, send_sem=halo_send.at[v, part],
+                        recv_sem=halo_recv.at[v, part], device_id=to,
+                        device_id_type=MESH).start()
 
     near = [jnp.where(inside[k][-1], 1, 0) + jnp.where(inside[k][1], 1, 0) for k in range(3)]
     cases = [(0,) if n == 1 else (1,) if n == 2 else (1, 2) for n in sizes]
 
     def halo_wait(v, part):
-        m = 0 if part is sides else 1
-        for a in ((0,) if part is sides else cases[0]):
-            for b in cases[1]:
-                for c in cases[2]:
-                    rows = b * nx + c * (1 + b) if part is sides else a * (
-                        ny + b + c * (1 + b))
+        for a in ((0,) if part == SIDES else cases[0]):
+            for b in (0,) if part == LAST else cases[1]:
+                for c in (0,) if part == LAST else cases[2]:
+                    edges = b + c * (1 + b)
+                    rows = (b * nx + c * (1 + b), a * (split + edges), a * (ny - split))[part]
                     if not rows:
                         continue
-                    flag = jnp.logical_and(near[1] == b, near[2] == c)
-                    if part is faces:
-                        flag = jnp.logical_and(flag, near[0] == a)
+                    known = []
+                    if part != SIDES:
+                        known.append(near[0] == a)
+                    if part != LAST:
+                        known += [near[1] == b, near[2] == c]
+                    flag = known[0]
+                    for more in known[1:]:
+                        flag = jnp.logical_and(flag, more)
 
                     @pl.when(flag)
                     def _(rows=rows):
                         some = bytes_of.at[pl.ds(0, rows)]
-                        for sem in (halo_recv.at[v, m], halo_send.at[v, m]):
+                        for sem in (halo_recv.at[v, part], halo_send.at[v, part]):
                             pltpu.make_async_copy(some, some, sem).wait()
 
     def total(value):
@@ -178,7 +190,7 @@
         return jnp.where(first_lanes, first, jnp.where(last_lanes, last, middle))
 
     def collect(v, part):
-        for dx in (0,) if part is sides else (-1, 1):
+        for dx in (0,) if part == SIDES else (-1, 1):
             low, high = [[edge_in[v, code((-dx, -dy, -dz))] for dy in (-1, 0, 1)]
                          for dz in (-1, 1)]
             for x in range(1, nx + 1) if dx == 0 else (0,) if dx < 0 else (nx + 1,):
@@ -197,7 +209,8 @@
                           jnp.where(odd, high_z, low_z), 0)
 
     def build(tile_of, shifted, turn, part):
-        inner = part is sides
+        inner = part == SIDES
+        rows = (range(wide), range(split + 1), range(split + 1, wide))[part]
 
         def step(i, carry):
             if inner:
@@ -214,7 +227,7 @@
             least = 1 if inner else jnp.where(x_ok, 1, 2)
             edge = tile_of(x, wide, inner)
             edge = jnp.where(keep_edge >= least, edge, jnp.zeros_like(edge)).astype(bf16)
-            for y in range(wide):
+            for y in rows:
                 tile = tile_of(x, y, inner)
                 limit = limits.get(y, middle)
                 if limit is not None:
@@ -259,24 +272,31 @@
                 [shifted[(x + a) * wide + y + yi] for x in range(nx)], axis=1))
         return parts
 
-    def conv_rows(shifted, w, finish, init):
-        def step(i, carry):
-            y0 = i * DEEP
-            data = jnp.concatenate(
-                [p for a in range(3) for p in stack_rows(shifted, a, y0, DEEP)], axis=0)
-            o = jnp.dot(mats[w], data, preferred_element_type=f32)
-            for x in range(nx):
-                for u in range(DEEP):
-                    carry = finish(
-                        x, y0 + u, o[u * chan:(u + 1) * chan, x * nz:(x + 1) * nz], carry)
-            return carry
-        return lax.fori_loop(0, ny // DEEP, step, init, unroll=2)
-
-    def conv_stats(shifted, w, full):
+    def conv_rows(shifted, w, finish, carry, between):
+        groups = ny // DEEP
+        for half in range(2):
+            def step(i, carry):
+                y0 = i * DEEP
+                data = jnp.concatenate(
+                    [p for a in range(3) for p in stack_rows(shifted, a, y0, DEEP)], axis=0)
+                o = jnp.dot(mats[w], data, preferred_element_type=f32)
+                for x in range(nx):
+                    for u in range(DEEP):
+                        carry = finish(
+                            x, y0 + u, o[u * chan:(u + 1) * chan, x * nz:(x + 1) * nz], carry)
+                return carry
+            if half:
+                between()
+            carry = lax.fori_loop(
+                half * (groups // 2), groups // 2 if half == 0 else groups, step, carry,
+                unroll=2)
+        return carry
+
+    def conv_stats(shifted, w, full, between):
         def finish(x, y, o, carry):
             full[x, y] = o
             return carry[0] + o, carry[1] + o * o
-        return conv_rows(shifted, w, finish, (zero, zero))
+        return conv_rows(shifted, w, finish, (zero, zero), between)
 
     def row_of(values):
         tile = zero
@@ -327,7 +347,7 @@
     def set_offsets(k, j, mean, part):
         def off(offset):
             return rounded(column(slots[j, rank_of(at_offset(offset))], 0)) - mean
-        for dx in (0,) if part is sides else (-1, 1):
+        for dx in (0,) if part == SIDES else (-1, 1):
             rows = [-mean if dx == 0 and dy == 0 else off((dx, dy, 0)) for dy in (-1, 0, 1)]
             edges = by_row(*[jnp.where(odd, off((dx, dy, 1)), off((dx, dy, -1)))
                              for dy in (-1, 0, 1)])
@@ -336,59 +356,75 @@
                     offs[k, x, kind] = value
 
     plane = sizes[1] * sizes[2]
+    assert plane >= tiles
     in_plane = lax.rem(rank, plane)
+    owner = in_plane < tiles
     plane_others = [o for o in others if o[0] == 0]
     line_others = [o for o in others if o[1] == 0 and o[2] == 0]
 
-    def pieces():
-        for u in range(tiles * (chan // 8)):
-            r, t = u // tiles, u % tiles
-            yield u // units, (u % units) * 8, r, t
-
-    def send_some(group, src_of, buf, at, send, recv):
+    def send_some(group, src, dst, send, recv):
         for offset in group:
-            to = at_offset(offset)
             pltpu.make_async_remote_copy(
-                src_ref=src_of(to), dst_ref=buf.at[at], send_sem=send,
-                recv_sem=recv, device_id=ids(to), device_id_type=MESH).start()
-
-    def plane_start(j, unit, slot, with_x=False):
-        for place, at, r, t in pieces():
-            unit[place, pl.ds(at, 8)] = wsum[
-                r * 8:r * 8 + 8, t * nz:(t + 1) * nz].astype(unit.dtype)
-        if with_x:
-            for place in range(plane):
-                for t in range(tiles):
-                    unit[place, pl.ds(8 * units + t, 1)] = xsum[:, t * nz:(t + 1) * nz]
-        slot[in_plane] = unit[in_plane]
-        send_some(plane_others, lambda to: unit.at[to[1] * sizes[2] + to[2]], slot, in_plane,
-                  w_send.at[j], w_recv.at[j])
-
-    def added(j, buf, n):
-        wait_bytes(buf, n, w_recv.at[j], w_send.at[j])
+                src_ref=src, dst_ref=dst, send_sem=send, recv_sem=recv,
+                device_id=ids(at_offset(offset)), device_id_type=MESH).start()
+
+    def plane_start(j, unit, slot):
+        for t in range(tiles):
+            unit[t, 0:chan] = wsum[:, t * nz:(t + 1) * nz].astype(unit.dtype)
+            if unit.shape[1] > chan:
+                unit[t, chan:chan + 1] = xsum[:, t * nz:(t + 1) * nz]
+        for t in range(tiles):
+            @pl.when(in_plane != t)
+            def _(t=t):
+                pltpu.make_async_remote_copy(
+                    src_ref=unit.at[t], dst_ref=slot.at[in_plane], send_sem=w_send.at[j],
+                    recv_sem=w_recv.at[j], device_id_type=MESH,
+                    device_id={AXES[1]: t // sizes[2], AXES[2]: t % sizes[2]}).start()
+
+        @pl.when(owner)
+        def _():
+            slot[in_plane] = unit[in_plane]
+
+    def added(buf, n):
         return tree([buf[r].astype(f32) for r in range(n)])
 
-    def line_start(j, slot, line):
-        line[me[0]] = added(j, slot, plane).astype(line.dtype)
-        send_some(line_others, lambda to: line.at[me[0]], line, me[0],
-                  w_send.at[j + 1], w_recv.at[j + 1])
-
-    def line_finish(j, line):
-        return added(j + 1, line, sizes[0])
+    def line_start(j, unit, slot, line):
+        @pl.when(owner)
+        def _():
+            wait_bytes(slot, plane, w_recv.at[j])
+            wait_bytes(unit, tiles, w_send.at[j])
+            line[me[0]] = added(slot, plane).astype(line.dtype)
+            here = line.at[me[0]]
+            send_some(line_others, here, here, w_send.at[j + 1], w_recv.at[j + 1])
+
+        @pl.when(jnp.logical_not(owner))
+        def _():
+            wait_bytes(unit, tiles + 1, w_send.at[j])
+
+    def line_sum(j, line):
+        wait_bytes(line, sizes[0], w_recv.at[j + 1], w_send.at[j + 1])
+        return added(line, sizes[0])
 
     def share(j, value):
         wfull[j, in_plane] = value.astype(bf16)
-        send_some(plane_others, lambda to: wfull.at[j, in_plane], wfull.at[j], in_plane,
-                  w_send.at[j], w_recv.at[j])
+        here = wfull.at[j, in_plane]
+        send_some(plane_others, here, here, w_send.at[j], w_recv.at[j])
 
     def spell(j, out):
-        wait_bytes(wfull.at[j], plane, w_recv.at[j], w_send.at[j])
-        for place, at, r, t in pieces():
-            piece = wfull[j, place, pl.ds(at, 8)].astype(f32)
+        @pl.when(owner)
+        def _():
+            wait_bytes(wfull.at[j], tiles, w_recv.at[j])
+            wait_bytes(wfull.at[j], plane, w_send.at[j])
+
+        @pl.when(jnp.logical_not(owner))
+        def _():
+            wait_bytes(wfull.at[j], tiles + 1, w_recv.at[j])
+        for t in range(tiles):
+            piece = wfull[j, t].astype(f32)
             for k in range(nz // chan):
                 tap = t * (nz // chan) + k
                 if tap < 27:
-                    out[tap, pl.ds(r * 8, 8)] = piece[:, k * chan:(k + 1) * chan]
+                    out[tap] = piece[:, k * chan:(k + 1) * chan]
 
     def wgrad(delta_of, shifted, ones=False):
         cuts = []
@@ -476,20 +512,25 @@
         return spread(column(value, 0))
     gain_one, bias_one, gain_two, bias_two = [gain(k) for k in range(4)]
 
-    for part in (sides, faces):
-        halo_wait(XB, part)
-        collect(XB, part)
-        build(raw_tiles(XB), shift_xb, False, part)
-    sums = conv_stats(shift_xb, 0, c1b)
+    def bring(v, shifted, tile_of, part, ready=None):
+        if part != LAST and ready is not None:
+            ready(part)
+        halo_wait(v, part)
+        if part != LAST:
+            collect(v, part)
+        build(tile_of, shifted, False, part)
+
+    def bring_conv(v, shifted, tile_of, w, full, ready=None):
+        bring(v, shifted, tile_of, SIDES, ready)
+        bring(v, shifted, tile_of, FIRST, ready)
+        return conv_stats(shifted, w, full, lambda: bring(v, shifted, tile_of, LAST))
+
+    sums = bring_conv(XB, shift_xb, raw_tiles(XB), 0, c1b)
     sums_start(0, sums)
     emit(C1B, lambda x, y: c1b[x, y], centre_of(sums))
     halo_start(C1B)
 
-    for part in (sides, faces):
-        halo_wait(XA, part)
-        collect(XA, part)
-        build(raw_tiles(XA), shift_a, False, part)
-    sums = conv_stats(shift_a, 0, c1a)
+    sums = bring_conv(XA, shift_a, raw_tiles(XA), 0, c1a)
     sums_start(1, sums)
     emit(C1A, lambda x, y: c1a[x, y], centre_of(sums))
     halo_start(C1A)
@@ -503,12 +544,8 @@
 
     def z_one(x, y, inner):
         return tile_1b(x, y, inner) * steep_one + bias_one
-    for part in (sides, faces):
-        set_offsets(0, 0, mean_one, part)
-        halo_wait(C1B, part)
-        collect(C1B, part)
-        build(lambda *at: silu(z_one(*at)), shift_hb, False, part)
-    sums = conv_stats(shift_hb, 2, c2b)
+    sums = bring_conv(C1B, shift_hb, lambda *at: silu(z_one(*at)), 2, c2b,
+                      lambda part: set_offsets(0, 0, mean_one, part))
     sums_start(2, sums)
     emit(C2B, lambda x, y: c2b[x, y], centre_of(sums))
     halo_start(C2B)
@@ -516,12 +553,8 @@
     mean_a, scale_a = norm(sums_finish(1))
     steep_a = gain_one * scale_a
     tile_1a = centred(C1A, 1, c1a)
-    for part in (sides, faces):
-        set_offsets(1, 1, mean_a, part)
-        halo_wait(C1A, part)
-        collect(C1A, part)
-        build(lambda *at: silu(tile_1a(*at) * steep_a + bias_one), shift_a, False, part)
-    sums = conv_stats(shift_a, 2, c2a)
+    sums = bring_conv(C1A, shift_a, lambda *at: silu(tile_1a(*at) * steep_a + bias_one), 2,
+                      c2a, lambda part: set_offsets(1, 1, mean_a, part))
     sums_start(3, sums)
 
     mean_two, scale_two = norm(sums_finish(2))
@@ -539,8 +572,9 @@
     sums_start(4, (sx * scale_two, sd))
     halo_start(GO)
 
-    wgrad(lambda x, y: ((c1b[x, y] - mean_one) * scale_one).astype(bf16), shift_xb, True)
-    plane_start(2, unit_x, slot_x, True)
+    wgrad(lambda x, y: ((c1b[x, y] - mean_one) * scale_one).astype(bf16), shift_xb,
+          True)
+    plane_start(2, unit_x, slot_x)
 
     tile_2b = centred(C2B, 2, c2b)
     tile_go = raw_tiles(GO)
@@ -551,17 +585,18 @@
     def halo_two(x, y, inner):
         fd2[x, y] = d_two(x, y, inner)
 
-    set_offsets(2, 2, mean_two, sides)
-    halo_wait(C2B, sides)
-    collect(C2B, sides)
-    halo_wait(GO, sides)
-    collect(GO, sides)
+    set_offsets(2, 2, mean_two, SIDES)
+    halo_wait(C2B, SIDES)
+    collect(C2B, SIDES)
+    halo_wait(GO, SIDES)
+    collect(GO, SIDES)
     halo_rows(halo_two)
     for x in range(1, nx + 1):
         dcols[D2, x] = d_two(x, wide, True)
-    set_offsets(2, 2, mean_two, faces)
-    halo_wait(C2B, faces)
-    collect(C2B, faces)
+    set_offsets(2, 2, mean_two, FIRST)
+    halo_wait(C2B, FIRST)
+    collect(C2B, FIRST)
+    halo_wait(C2B, LAST)
 
     mean_a2, scale_a2 = norm(sums_finish(3))
     steep_a2 = gain_two * scale_a2
@@ -584,10 +619,15 @@
         else:
             d = dcols[D2, x] if y == wide else fd2[x, y]
         return steep_two * (d - sd2 - c * sx2)
-    build(dc_two, shift_d, True, sides)
-    halo_wait(GO, faces)
-    collect(GO, faces)
-    build(dc_two, shift_d, True, faces)
+    build(dc_two, shift_d, True, SIDES)
+    halo_wait(GO, FIRST)
+    collect(GO, FIRST)
+    build(dc_two, shift_d, True, FIRST)
+
+    def rest_two():
+        line_start(2, unit_x, slot_x, line_x)
+        halo_wait(GO, LAST)
+        build(dc_two, shift_d, True, LAST)
 
     def back(x, y, o, carry):
         sd, sx = carry
@@ -597,13 +637,12 @@
         fd1[x + 1, y + 1] = d
         d1h[x, y] = d.astype(bf16)
         return sd + d, sx + d * c
-    sd, sx = conv_rows(shift_d, 3, back, (zero, zero))
+    sd, sx = conv_rows(shift_d, 3, back, (zero, zero), rest_two)
     sums_start(5, (sx * scale_one, sd))
     emit(E1, lambda x, y: e1[x, y])
     halo_start(E1)
     wgrad(lambda x, y: d1h[x, y], shift_xb)
     plane_start(4, unit_f, slot_f)
-    line_start(2, slot_x, line_x)
     wgrad(lambda x, y: shift_d[(x + 1) * wide + y + 1, chan:2 * chan], shift_hb)
     plane_start(6, unit_h, slot_h)
 
@@ -611,9 +650,7 @@
     sx1_wide = spread(column(row_one, 0) / voxels)
     sx1 = sx1_wide * scale_one
     sd1 = spread(column(row_one, 1) / voxels)
-    for k, value in enumerate((steep_one * factor, sd1, sx1_wide)):
-        kcol[k] = value
-
+    line_start(4, unit_f, slot_f, line_f)
     def halo_one(x, y, inner):
         fd1[x, y] = pads[E1, x, y].astype(f32) * slope_of(z_one(x, y, inner))
 
@@ -626,38 +663,34 @@
             d = e.astype(f32) * slope_of(c * steep_one + bias_one)
         return steep_one * (d - sd1 - c * sx1)
 
-    halo_wait(E1, sides)
-    collect(E1, sides)
+    halo_wait(E1, SIDES)
+    collect(E1, SIDES)
     halo_rows(halo_one)
     for x in range(1, nx + 1):
         dcols[D1, x] = cols[E1, x].astype(f32) * slope_of(z_one(x, wide, True))
-    build(dc_one, shift_d, True, sides)
-
-    line_start(4, slot_f, line_f)
-
-    halo_wait(E1, faces)
-    collect(E1, faces)
-    build(dc_one, shift_d, True, faces)
-    line_start(6, slot_h, line_h)
+    build(dc_one, shift_d, True, SIDES)
+
+    halo_wait(E1, FIRST)
+    collect(E1, FIRST)
+    build(dc_one, shift_d, True, FIRST)
+    line_start(6, unit_h, slot_h, line_h)
+
+    def rest_one():
+        halo_wait(E1, LAST)
+        build(dc_one, shift_d, True, LAST)
 
     def last(x, y, o, carry):
         put_row(x, y, o)
         return carry
-    conv_rows(shift_d, 1, last, 0)
+    conv_rows(shift_d, 1, last, 0, rest_one)
     give(dxb)
-    along = line_finish(2, line_x)
-    plain[...] = along[8 * units:]
-    straight = line_finish(4, line_f)
-    mixed = []
-    for q in range(units):
-        u = in_plane * units + q
-        r = pl.multiple_of(jnp.minimum(lax.div(u, tiles), chan // 8 - 1) * 8, 8)
-        k, d, x = [kcol[i, pl.ds(r, 8)] for i in range(3)]
-        part = slice(q * 8, q * 8 + 8)
-        mixed.append(k * (straight[part] - d * plain[pl.ds(lax.rem(u, tiles), 1)]
-                          - x * along[part]))
-    share(0, jnp.concatenate(mixed, axis=0))
-    share(1, line_finish(6, line_h) * factor)
+
+    @pl.when(owner)
+    def _():
+        along = line_sum(2, line_x)
+        share(0, steep_one * factor * (
+            line_sum(4, line_f) - sd1 * along[chan:chan + 1] - sx1_wide * along[0:chan]))
+        share(1, line_sum(6, line_h) * factor)
     for k, row in enumerate((row_one, row_two)):
         for j in range(2):
             gnorm[2 * k + j:2 * k + j + 1, :] = row[:, j * chan:(j + 1) * chan] * factor
@@ -685,7 +718,6 @@
     bf16, f32 = jnp.bfloat16, jnp.float32
     tiles = -(-taps // nz)
     plane = sizes[1] * sizes[2]
-    units = -(-tiles * (chan // 8) // plane)
     full = (nx + 2, ny + 2, chan, nz)
     span = (nx + 2) * (ny + 2)
     grid = (nx, ny, chan, nz)
@@ -700,7 +732,7 @@
         jax.ShapeDtypeStruct((4, chan), f32),
     )
     results = pl.pallas_call(
-        functools.partial(kernel, sizes, voxels, units),
+        functools.partial(kernel, sizes, voxels),
         out_shape=shapes,
         in_specs=[hbm] * 9,
         out_specs=[vmem] * 5,
@@ -723,22 +755,20 @@
             pltpu.VMEM(grid, bf16),
             pltpu.VMEM((6, count, 1, nz), f32),
             pltpu.VMEM((1, tiles * nz), f32),
-            pltpu.VMEM((8, nz), f32),
-            pltpu.VMEM((3, chan, nz), f32),
             pltpu.VMEM((chan, tiles * nz), f32),
-            pltpu.VMEM((plane, 8 * units + 8, nz), f32),
-            pltpu.VMEM((plane, 8 * units + 8, nz), f32),
-            pltpu.VMEM((sizes[0], 8 * units + 8, nz), f32),
-            pltpu.VMEM((plane, 8 * units, nz), f32),
-            pltpu.VMEM((plane, 8 * units, nz), f32),
-            pltpu.VMEM((sizes[0], 8 * units, nz), f32),
-            pltpu.VMEM((plane, 8 * units, nz), bf16),
-            pltpu.VMEM((plane, 8 * units, nz), bf16),
-            pltpu.VMEM((sizes[0], 8 * units, nz), bf16),
-            pltpu.VMEM((2, plane, 8 * units, nz), bf16),
+            pltpu.VMEM((tiles + 1, chan + 8, nz), f32),
+            pltpu.VMEM((plane, chan + 8, nz), f32),
+            pltpu.VMEM((sizes[0], chan + 8, nz), f32),
+            pltpu.VMEM((tiles + 1, chan, nz), f32),
+            pltpu.VMEM((plane, chan, nz), f32),
+            pltpu.VMEM((sizes[0], chan, nz), f32),
+            pltpu.VMEM((tiles + 1, chan, nz), bf16),
+            pltpu.VMEM((plane, chan, nz), bf16),
+            pltpu.VMEM((sizes[0], chan, nz), bf16),
+            pltpu.VMEM((2, plane + 1, chan, nz), bf16),
             pltpu.VMEM((2 * (ny + 8), chan, nz), bf16),
             dma((9,)),
-            dma((7, 2)), dma((7, 2)),
+            dma((7, 3)), dma((7, 3)),
             dma((6,)), dma((6,)),
             dma((8,)), dma((8,)),
         ],

time: 51.4 us -> 50.4 us (0.981)
  Pallas kernels: 50.4 us -> 49.4 us
    pallas_call x1, Pallas kernels: 49.3 us -> 48.3 us  [body(): pl.pallas_call(functools.partial(kernel, sizes, voxels), out_shape=shapes...]
where the time goes in v5:
time: 50.4 us; the launch traced here: 50.2 us
  Pallas kernels  49.4 us (98%)
  between operations  0.8 us (2%)
    pallas_call x1, Pallas kernels, body(): pl.pallas_call(functools.partial(kernel, sizes, voxels), out_shape=shapes...  48.3 us
    pallas_call x1, Pallas kernels, body(): pl.pallas_call(deliver, out_shape=shapes, in_specs=[vmem] * 5, out_specs=...  1.13 us

profile of v5, /device:TPU:0, one launch (start us, length us, event | category | flops | bytes accessed | tf_op | source)
XLA Modules:
  0.0 50.2 jit_solution(400750267137724906)
XLA Ops:
  0.6 48.3 %shard_map.128 = (bf16[32,2,16,128]{3,2,1,0:T(8,128)(2,1)S(1)}, bf16[32,2,16,128]{3,2,1,0:T(8,128)(2,1)S(1)}, f32[27,32,32]{2,1,0:T(8,128)S(1)}, f32[27,32,32]{2,1,0:T(8,128)S(1)}, f32[4,32]{1,0:T(4,128)S(1)}) custom-call(bf16[32,2,16,128]{3,2,1,0:T(8,128)(2,1)} %xa.1, bf16[32,2,16,128]{3,2,1,0:T(8,128)(2,1)} %xb.1, bf16[32,2,16,128]{3,2,1,0:T(8,128)(2,1)} %go.1, ...), custom_call_target="tpu_custom_call" | custom-call | tf_op jit(solution)/shard_map/pallas_call | solution.py:734
  48.9 1.1 %shard_map.129 = (bf16[32,2,16,128]{3,2,1,0:T(8,128)(2,1)}, bf16[32,2,16,128]{3,2,1,0:T(8,128)(2,1)}, f32[27,32,32]{2,1,0:T(8,128)}, f32[27,32,32]{2,1,0:T(8,128)}, f32[4,32]{1,0:T(4,128)}) custom-call(bf16[32,2,16,128]{3,2,1,0:T(8,128)(2,1)S(1)} %get-tuple-element.15.refs_0_, bf16[32,2,16,128]{3,2,1,0:T(8,128)(2,1)S(1)} %get-tuple-element.16.refs_1_, ...), custom_call_target="tpu_custom_call" | custom-call | tf_op jit(solution)/shard_map/pallas_call | solution.py:783

commit v6 on v5

--- a/solution.py
+++ b/solution.py
@@ -42,7 +42,7 @@
     ya, dxb, gw1, gw2, gnorm,
     raw, wraw, gains, tall, mats, pads, edge_out, edge_in, cols, dcols, offs,
     shift_xb, shift_a, shift_hb, shift_d,
-    fd2, fd1, c1b, c1a, c2b, c2a, e1, d1h, slots, xsum, wsum,
+    fd2, fd1, c1b, c1a, c2b, c2a, d1h, slots, xsum, wsum,
     unit_x, slot_x, line_x, unit_f, slot_f, line_f, unit_h, slot_h, line_h, wfull,
     bytes_of, load_sem, halo_send, halo_recv, sum_send, sum_recv, w_send, w_recv,
 ):
@@ -68,16 +68,13 @@
     others = [(a, b, c) for a in range(sizes[0]) for b in range(sizes[1])
               for c in range(sizes[2])][:0:-1]
 
+    places = [{o: lax.rem(m + o + s, s) for o in range(-1, s)} for m, s in zip(me, sizes)]
+
     def at_offset(offset):
-        return [lax.rem(m + o + s, s) for m, o, s in zip(me, offset, sizes)]
+        return [places[k][o] for k, o in enumerate(offset)]
 
     def ids(place):
         return dict(zip(AXES, place))
-
-    barrier = pltpu.get_barrier_semaphore()
-    for offset in others:
-        pl.semaphore_signal(
-            barrier, inc=1, device_id=ids(at_offset(offset)), device_id_type=MESH)
 
     loads = []
     for at, (src, dst) in enumerate((
@@ -87,6 +84,11 @@
         copy = pltpu.make_async_copy(src, dst, load_sem.at[at])
         copy.start()
         loads.append(copy)
+
+    barrier = pltpu.get_barrier_semaphore()
+    for offset in others:
+        pl.semaphore_signal(
+            barrier, inc=1, device_id=ids(at_offset(offset)), device_id_type=MESH)
 
     inside = []
     for k in range(3):
@@ -169,19 +171,21 @@
         by = by % nz
         return pltpu.roll(tile, by, 1) if by else tile
 
-    def emit(v, tile_of, centre=None):
+    def put(v, x, y, tile, edge):
+        tile = tile.astype(bf16)
+        pads[v, x + 1, y + 1] = tile
+        r = 2 * (x * ny + y)
+        edge = jnp.where(lane == r, tile[:, nz - 1:nz], edge)
+        return jnp.where(lane == r + 1, tile[:, 0:1], edge)
+
+    blank = jnp.zeros((chan, nz), bf16)
+
+    def emit(v, tile_of):
         def step(x, edge):
             for y in range(ny):
-                tile = tile_of(x, y)
-                if centre is not None:
-                    tile = tile - centre
-                tile = tile.astype(bf16)
-                pads[v, x + 1, y + 1] = tile
-                r = 2 * (x * ny + y)
-                edge = jnp.where(lane == r, tile[:, nz - 1:nz], edge)
-                edge = jnp.where(lane == r + 1, tile[:, 0:1], edge)
+                edge = put(v, x, y, tile_of(x, y), edge)
             return edge
-        edge_out[v] = lax.fori_loop(0, nx, step, zero.astype(bf16))
+        edge_out[v] = lax.fori_loop(0, nx, step, blank)
 
     first_lanes = jnp.logical_or(lane == 0, lane == nz - 1)
     last_lanes = jnp.logical_or(lane == 2 * ny + 1, lane == 2 * ny + 2)
@@ -283,20 +287,41 @@
                 for x in range(nx):
                     for u in range(DEEP):
                         carry = finish(
-                            x, y0 + u, o[u * chan:(u + 1) * chan, x * nz:(x + 1) * nz], carry)
+                            x, y0 + u, o[u * chan:(u + 1) * chan, x * nz:(x + 1) * nz],
+                            carry, half)
                 return carry
             if half:
-                between()
+                carry = between(carry)
             carry = lax.fori_loop(
                 half * (groups // 2), groups // 2 if half == 0 else groups, step, carry,
                 unroll=2)
         return carry
 
-    def conv_stats(shifted, w, full, between):
-        def finish(x, y, o, carry):
+    def conv_stats(v, shifted, w, full, between):
+        centre = []
+
+        def finish(x, y, o, carry, half):
             full[x, y] = o
-            return carry[0] + o, carry[1] + o * o
-        return conv_rows(shifted, w, finish, (zero, zero), between)
+            first, second, edge = carry
+            if half and v is not None:
+                edge = put(v, x, y, o - centre[0], edge)
+            return first + o, second + o * o, edge
+
+        def middle(carry):
+            first, second, edge = carry
+            if v is not None:
+                mean = spread(total(first) / (0.5 * local))
+                centre.append(mean.astype(bf16).astype(f32))
+                for x in range(nx):
+                    for y in range(ny // 2):
+                        edge = put(v, x, y, full[x, y] - centre[0], edge)
+            between()
+            return first, second, edge
+        first, second, edge = conv_rows(shifted, w, finish, (zero, zero, blank), middle)
+        if v is None:
+            return total(first), total(second)
+        edge_out[v] = edge
+        return total(first), total(second), centre[0]
 
     def row_of(values):
         tile = zero
@@ -326,7 +351,7 @@
         return values[0]
 
     def sums_start(j, values):
-        all_start(slots.at[j], row_of([total(v) for v in values]), sum_send.at[j],
+        all_start(slots.at[j], row_of(values), sum_send.at[j],
                   sum_recv.at[j])
 
     def sums_finish(j):
@@ -338,15 +363,9 @@
         var = column(row, 1) / voxels - mean * mean
         return spread(mean), spread(lax.rsqrt(var + EPSILON))
 
-    def rounded(value):
-        return spread(value / local).astype(bf16).astype(f32)
-
-    def centre_of(sums):
-        return rounded(total(sums[0]))
-
     def set_offsets(k, j, mean, part):
         def off(offset):
-            return rounded(column(slots[j, rank_of(at_offset(offset))], 0)) - mean
+            return spread(column(slots[j, rank_of(at_offset(offset))], 2)) - mean
         for dx in (0,) if part == SIDES else (-1, 1):
             rows = [-mean if dx == 0 and dy == 0 else off((dx, dy, 0)) for dy in (-1, 0, 1)]
             edges = by_row(*[jnp.where(odd, off((dx, dy, 1)), off((dx, dy, -1)))
@@ -436,21 +455,23 @@
                 cuts.append(jnp.concatenate(parts, axis=0))
         delta = jnp.concatenate(cuts, axis=1)
         span = 3 * chan
+        band = (DEEP + 2) * span
+        groups = [jnp.concatenate(
+            [p for a in range(3) for p in stack_rows(shifted, a, g * DEEP, DEEP)], axis=0)
+            for g in range(ny // DEEP)]
+        o = lax.dot_general(
+            delta, jnp.concatenate(groups, axis=1), (((1,), (1,)), ((), ())),
+            preferred_element_type=f32)
         for a in range(3):
-            groups = [jnp.concatenate(stack_rows(shifted, a, g * DEEP, DEEP), axis=0)
-                      for g in range(ny // DEEP)]
-            o = lax.dot_general(
-                delta, jnp.concatenate(groups, axis=1), (((1,), (1,)), ((), ())),
-                preferred_element_type=f32)
             for ty in range(3):
                 at = (a * 3 + ty) * span
+                spots = [a * band + (u + ty) * span for u in range(DEEP)]
                 wsum[:, at:at + span] = tree(
-                    [o[u * chan:(u + 1) * chan, (u + ty) * span:(u + ty + 1) * span]
-                     for u in range(DEEP)])
+                    [o[u * chan:(u + 1) * chan, spot:spot + span]
+                     for u, spot in enumerate(spots)])
                 if ones:
                     xsum[:, at:at + span] = tree(
-                        [o[DEEP * chan:DEEP * chan + 1, (u + ty) * span:(u + ty + 1) * span]
-                         for u in range(DEEP)])
+                        [o[DEEP * chan:DEEP * chan + 1, spot:spot + span] for spot in spots])
 
     def take(k):
         def step(c, carry):
@@ -520,19 +541,17 @@
             collect(v, part)
         build(tile_of, shifted, False, part)
 
-    def bring_conv(v, shifted, tile_of, w, full, ready=None):
+    def bring_conv(v, shifted, tile_of, w, full, out, ready=None):
         bring(v, shifted, tile_of, SIDES, ready)
         bring(v, shifted, tile_of, FIRST, ready)
-        return conv_stats(shifted, w, full, lambda: bring(v, shifted, tile_of, LAST))
-
-    sums = bring_conv(XB, shift_xb, raw_tiles(XB), 0, c1b)
+        return conv_stats(out, shifted, w, full, lambda: bring(v, shifted, tile_of, LAST))
+
+    sums = bring_conv(XB, shift_xb, raw_tiles(XB), 0, c1b, C1B)
     sums_start(0, sums)
-    emit(C1B, lambda x, y: c1b[x, y], centre_of(sums))
     halo_start(C1B)
 
-    sums = bring_conv(XA, shift_a, raw_tiles(XA), 0, c1a)
+    sums = bring_conv(XA, shift_a, raw_tiles(XA), 0, c1a, C1A)
     sums_start(1, sums)
-    emit(C1A, lambda x, y: c1a[x, y], centre_of(sums))
     halo_start(C1A)
 
     def silu(z):
@@ -544,17 +563,16 @@
 
     def z_one(x, y, inner):
         return tile_1b(x, y, inner) * steep_one + bias_one
-    sums = bring_conv(C1B, shift_hb, lambda *at: silu(z_one(*at)), 2, c2b,
+    sums = bring_conv(C1B, shift_hb, lambda *at: silu(z_one(*at)), 2, c2b, C2B,
                       lambda part: set_offsets(0, 0, mean_one, part))
     sums_start(2, sums)
-    emit(C2B, lambda x, y: c2b[x, y], centre_of(sums))
     halo_start(C2B)
 
     mean_a, scale_a = norm(sums_finish(1))
     steep_a = gain_one * scale_a
     tile_1a = centred(C1A, 1, c1a)
     sums = bring_conv(C1A, shift_a, lambda *at: silu(tile_1a(*at) * steep_a + bias_one), 2,
-                      c2a, lambda part: set_offsets(1, 1, mean_a, part))
+                      c2a, None, lambda part: set_offsets(1, 1, mean_a, part))
     sums_start(3, sums)
 
     mean_two, scale_two = norm(sums_finish(2))
@@ -569,7 +587,7 @@
             sd, sx = sd + d, sx + d * c
         return sd, sx
     sd, sx = lax.fori_loop(0, nx, own_two, (zero, zero))
-    sums_start(4, (sx * scale_two, sd))
+    sums_start(4, (total(sx * scale_two), total(sd)))
     halo_start(GO)
 
     wgrad(lambda x, y: ((c1b[x, y] - mean_one) * scale_one).astype(bf16), shift_xb,
@@ -625,24 +643,27 @@
     build(dc_two, shift_d, True, FIRST)
 
     def rest_two():
-        line_start(2, unit_x, slot_x, line_x)
         halo_wait(GO, LAST)
         build(dc_two, shift_d, True, LAST)
 
-    def back(x, y, o, carry):
-        sd, sx = carry
-        e1[x, y] = o
+    def back(x, y, o, carry, half):
+        sd, sx, edge = carry
         c = c1b[x, y] - mean_one
         d = o * slope_of(c * steep_one + bias_one)
         fd1[x + 1, y + 1] = d
         d1h[x, y] = d.astype(bf16)
-        return sd + d, sx + d * c
-    sd, sx = conv_rows(shift_d, 3, back, (zero, zero), rest_two)
-    sums_start(5, (sx * scale_one, sd))
-    emit(E1, lambda x, y: e1[x, y])
+        return sd + d, sx + d * c, put(E1, x, y, o, edge)
+
+    def rest_of_two(carry):
+        rest_two()
+        return carry
+    sd, sx, edge = conv_rows(shift_d, 3, back, (zero, zero, blank), rest_of_two)
+    edge_out[E1] = edge
+    sums_start(5, (total(sx * scale_one), total(sd)))
     halo_start(E1)
     wgrad(lambda x, y: d1h[x, y], shift_xb)
     plane_start(4, unit_f, slot_f)
+    line_start(2, unit_x, slot_x, line_x)
     wgrad(lambda x, y: shift_d[(x + 1) * wide + y + 1, chan:2 * chan], shift_hb)
     plane_start(6, unit_h, slot_h)
 
@@ -679,10 +700,14 @@
         halo_wait(E1, LAST)
         build(dc_one, shift_d, True, LAST)
 
-    def last(x, y, o, carry):
+    def last(x, y, o, carry, half):
         put_row(x, y, o)
         return carry
-    conv_rows(shift_d, 1, last, 0, rest_one)
+
+    def rest_of_one(carry):
+        rest_one()
+        return carry
+    conv_rows(shift_d, 1, last, 0, rest_of_one)
     give(dxb)
 
     @pl.when(owner)
@@ -750,7 +775,7 @@
             pltpu.VMEM((3, nx + 2, 4, chan, nz), f32),
         ] + [pltpu.VMEM((span, 3 * chan, nz), bf16)] * 4
         + [pltpu.VMEM(full, f32)] * 2
-        + [pltpu.VMEM(grid, f32)] * 5
+        + [pltpu.VMEM(grid, f32)] * 4
         + [
             pltpu.VMEM(grid, bf16),
             pltpu.VMEM((6, count, 1, nz), f32),

time: 50.4 us -> 50 us (level)
  no operation moved by 1% of the time
where the time goes in v6:
time: 50 us; the launch traced here: 49.9 us
  Pallas kernels  49.1 us (98%)
  between operations  0.8 us (2%)
    pallas_call x1, Pallas kernels, body(): pl.pallas_call(functools.partial(kernel, sizes, voxels), out_shape=shapes...  48 us
    pallas_call x1, Pallas kernels, body(): pl.pallas_call(deliver, out_shape=shapes, in_specs=[vmem] * 5, out_specs=...  1.13 us

profile of v6, /device:TPU:0, one launch (start us, length us, event | category | flops | bytes accessed | tf_op | source)
XLA Modules:
  0.0 49.9 jit_solution(15551503904524810834)
XLA Ops:
  0.6 48.0 %shard_map.128 = (bf16[32,2,16,128]{3,2,1,0:T(8,128)(2,1)S(1)}, bf16[32,2,16,128]{3,2,1,0:T(8,128)(2,1)S(1)}, f32[27,32,32]{2,1,0:T(8,128)S(1)}, f32[27,32,32]{2,1,0:T(8,128)S(1)}, f32[4,32]{1,0:T(4,128)S(1)}) custom-call(bf16[32,2,16,128]{3,2,1,0:T(8,128)(2,1)} %xa.1, bf16[32,2,16,128]{3,2,1,0:T(8,128)(2,1)} %xb.1, bf16[32,2,16,128]{3,2,1,0:T(8,128)(2,1)} %go.1, ...), custom_call_target="tpu_custom_call" | custom-call | tf_op jit(solution)/shard_map/pallas_call | solution.py:759
  48.6 1.1 %shard_map.129 = (bf16[32,2,16,128]{3,2,1,0:T(8,128)(2,1)}, bf16[32,2,16,128]{3,2,1,0:T(8,128)(2,1)}, f32[27,32,32]{2,1,0:T(8,128)}, f32[27,32,32]{2,1,0:T(8,128)}, f32[4,32]{1,0:T(4,128)}) custom-call(bf16[32,2,16,128]{3,2,1,0:T(8,128)(2,1)S(1)} %get-tuple-element.15.refs_0_, bf16[32,2,16,128]{3,2,1,0:T(8,128)(2,1)S(1)} %get-tuple-element.16.refs_1_, ...), custom_call_target="tpu_custom_call" | custom-call | tf_op jit(solution)/shard_map/pallas_call | solution.py:808

commit v7 on v6

--- a/solution.py
+++ b/solution.py
@@ -245,7 +245,7 @@
                 shifted[row, chan:2 * chan] = tile
                 shifted[row, 2 * chan:] = low if turn else high
             return carry
-        lax.fori_loop(0, nx if inner else 2, step, 0)
+        lax.fori_loop(0, nx if inner else 2, step, 0, unroll=2)
 
     def raw_tiles(v):
         def tile_of(x, y, inner):

time: 50 us -> 49.4 us (0.988)
  Pallas kernels: 49.1 us -> 48.5 us
    pallas_call x1, Pallas kernels: 48 us -> 47.4 us  [body(): pl.pallas_call(functools.partial(kernel, sizes, voxels), out_shape=shapes...]
where the time goes in v7:
time: 49.4 us; the launch traced here: 49.3 us
  Pallas kernels  48.5 us (98%)
  between operations  0.8 us (2%)
    pallas_call x1, Pallas kernels, body(): pl.pallas_call(functools.partial(kernel, sizes, voxels), out_shape=shapes...  47.4 us
    pallas_call x1, Pallas kernels, body(): pl.pallas_call(deliver, out_shape=shapes, in_specs=[vmem] * 5, out_specs=...  1.13 us

profile of v7, /device:TPU:0, one launch (start us, length us, event | category | flops | bytes accessed | tf_op | source)
XLA Modules:
  0.0 49.3 jit_solution(13812946950493195815)
XLA Ops:
  0.6 47.4 %shard_map.128 = (bf16[32,2,16,128]{3,2,1,0:T(8,128)(2,1)S(1)}, bf16[32,2,16,128]{3,2,1,0:T(8,128)(2,1)S(1)}, f32[27,32,32]{2,1,0:T(8,128)S(1)}, f32[27,32,32]{2,1,0:T(8,128)S(1)}, f32[4,32]{1,0:T(4,128)S(1)}) custom-call(bf16[32,2,16,128]{3,2,1,0:T(8,128)(2,1)} %xa.1, bf16[32,2,16,128]{3,2,1,0:T(8,128)(2,1)} %xb.1, bf16[32,2,16,128]{3,2,1,0:T(8,128)(2,1)} %go.1, ...), custom_call_target="tpu_custom_call" | custom-call | tf_op jit(solution)/shard_map/pallas_call | solution.py:759
  48.0 1.1 %shard_map.129 = (bf16[32,2,16,128]{3,2,1,0:T(8,128)(2,1)}, bf16[32,2,16,128]{3,2,1,0:T(8,128)(2,1)}, f32[27,32,32]{2,1,0:T(8,128)}, f32[27,32,32]{2,1,0:T(8,128)}, f32[4,32]{1,0:T(4,128)}) custom-call(bf16[32,2,16,128]{3,2,1,0:T(8,128)(2,1)S(1)} %get-tuple-element.15.refs_0_, bf16[32,2,16,128]{3,2,1,0:T(8,128)(2,1)S(1)} %get-tuple-element.16.refs_1_, ...), custom_call_target="tpu_custom_call" | custom-call | tf_op jit(solution)/shard_map/pallas_call | solution.py:808
